TPU v7x, 8 devices: a whole 2x2x1 slice. The times are simulated.
8 devices in a mesh: dp: 2 (over z, y), a: 4 (over x, core).
Axes of the slice: x: 2, y: 2, z: 1, core: 2. Of those that a mesh axis runs over, the one named last changes fastest.
Arguments:
- hidden_in: bfloat16 [16, 2560], P('dp'), parts along dimension 0
- loc_k: bfloat16 [16, 4, 6144, 256], P('dp', None, 'a'), parts along dimension 0
- loc_v: bfloat16 [16, 4, 6144, 256], P('dp', None, 'a'), parts along dimension 0
- glo_k: bfloat16 [16, 4, 6144, 256], P('dp', None, 'a'), parts along dimension 0
- glo_v: bfloat16 [16, 4, 6144, 256], P('dp', None, 'a'), parts along dimension 0
- loc_wq: bfloat16 [2560, 2048], P(None, 'a')
- loc_wk: bfloat16 [2560, 1024], P(None, 'a')
- loc_wv: bfloat16 [2560, 1024], P(None, 'a')
- loc_wo: bfloat16 [2048, 2560], P('a')
- loc_pre: bfloat16 [2560], replicated
- loc_post: bfloat16 [2560], replicated
- glo_wq: bfloat16 [2560, 2048], P(None, 'a')
- glo_wk: bfloat16 [2560, 1024], P(None, 'a')
- glo_wv: bfloat16 [2560, 1024], P(None, 'a')
- glo_wo: bfloat16 [2048, 2560], P('a')
- glo_pre: bfloat16 [2560], replicated
- glo_post: bfloat16 [2560], replicated
Outputs:
- output 1: bfloat16 [16, 2560], P('dp'), parts along dimension 0
- output 2: bfloat16 [16, 4, 4096, 256], P('dp', 'a'), parts along dimension 0
- output 3: bfloat16 [16, 4, 4096, 256], P('dp', 'a'), parts along dimension 0
- output 4: bfloat16 [16, 4, 6656, 256], P('dp', 'a'), parts along dimension 0
- output 5: bfloat16 [16, 4, 6656, 256], P('dp', 'a'), parts along dimension 0
There are 2 independent parts. A program takes and returns all parts, laid end to end along the dimension named above; an argument that names none is the same for every part.
All inputs are finite; a program needn't handle non-finite values.
Results may differ from a plain program's by a relative error of at most 0.02.
Values are sent between devices in bfloat16 or wider.
A program may use at most 1 GiB of HBM per device.

v0:
```python
import jax
import jax.numpy as jnp
from jax import lax
from jax.sharding import PartitionSpec as P, NamedSharding

SOFTCAP = 50.0
NORM_EPS = 1e-6
ROPE_BASE = 10000.0
WINDOW = 4096
CACHE_ROOM = 512


def rms_norm(hidden, gain):
    mean_sq = jnp.mean(hidden * hidden, axis=-1, keepdims=True)
    return hidden * lax.rsqrt(mean_sq + NORM_EPS) * (1.0 + gain.astype(jnp.float32))


def rope_at(heads, position):
    head_dim = heads.shape[-1]
    half_dim = head_dim // 2
    inv_freq = ROPE_BASE ** (-2.0 * jnp.arange(half_dim, dtype=jnp.float32) / head_dim)
    angles = position * inv_freq
    cosine = jnp.cos(angles)
    sine_val = jnp.sin(angles)
    first_half = heads[..., :half_dim]
    second_half = heads[..., half_dim:]
    return jnp.concatenate([first_half * cosine - second_half * sine_val, second_half * cosine + first_half * sine_val], axis=-1)


def attend(q_heads, old_k, old_v, new_k, new_v):
    q_scale = q_heads.shape[-1] ** -0.5
    old_scores = jnp.einsum('bkgd,bkld->bkgl', q_heads, old_k, preferred_element_type=jnp.float32) * q_scale
    new_scores = jnp.einsum('clhe,cle->clh', q_heads, new_k, preferred_element_type=jnp.float32) * q_scale
    old_scores = SOFTCAP * jnp.tanh(old_scores / SOFTCAP)
    new_scores = SOFTCAP * jnp.tanh(new_scores / SOFTCAP)
    top_score = jnp.maximum(jnp.max(old_scores, axis=-1), new_scores)
    old_weights = jnp.exp(old_scores - top_score[..., None])
    new_weights = jnp.exp(new_scores - top_score)
    denom_sum = jnp.sum(old_weights, axis=-1) + new_weights
    weighted = jnp.einsum('bkgl,bkld->bkgd', old_weights.astype(jnp.bfloat16), old_v, preferred_element_type=jnp.float32)
    weighted = weighted + new_weights.astype(jnp.bfloat16).astype(jnp.float32)[..., None] * new_v.astype(jnp.float32)[:, :, None, :]
    return weighted / denom_sum[..., None]


def decode_layer(hidden, cache_k, cache_v, w_q, w_k, w_v, w_o, pre_gain, post_gain, is_local):
    num_rows, kv_local, seq_len, head_dim = cache_k.shape
    heads_local = w_q.shape[1] // head_dim
    q_groups = heads_local // kv_local
    normed = rms_norm(hidden.astype(jnp.float32), pre_gain).astype(jnp.bfloat16)
    q_proj = jnp.dot(normed, w_q, preferred_element_type=jnp.float32)
    q_heads = rope_at(q_proj.reshape(num_rows, kv_local, q_groups, head_dim), seq_len).astype(jnp.bfloat16)
    k_proj = jnp.dot(normed, w_k, preferred_element_type=jnp.float32)
    new_k = rope_at(k_proj.reshape(num_rows, kv_local, head_dim), seq_len).astype(jnp.bfloat16)
    new_v = jnp.dot(normed, w_v, preferred_element_type=jnp.float32).astype(jnp.bfloat16).reshape(num_rows, kv_local, head_dim)
    if is_local:
        old_k = cache_k[:, :, seq_len - WINDOW + 1:]
        old_v = cache_v[:, :, seq_len - WINDOW + 1:]
        roll_shift = (seq_len + 1) % WINDOW
        out_k = jnp.roll(jnp.concatenate([old_k, new_k[:, :, None]], axis=2), roll_shift, axis=2)
        out_v = jnp.roll(jnp.concatenate([old_v, new_v[:, :, None]], axis=2), roll_shift, axis=2)
    else:
        old_k = cache_k
        old_v = cache_v
        zero_pad = jnp.zeros((num_rows, kv_local, CACHE_ROOM - 1, head_dim), jnp.bfloat16)
        out_k = jnp.concatenate([cache_k, new_k[:, :, None], zero_pad], axis=2)
        out_v = jnp.concatenate([cache_v, new_v[:, :, None], zero_pad], axis=2)
    weighted = attend(q_heads, old_k, old_v, new_k, new_v)
    attn_out = weighted.astype(jnp.bfloat16).reshape(num_rows, heads_local * head_dim)
    part_sum = jnp.dot(attn_out, w_o, preferred_element_type=jnp.float32).astype(jnp.bfloat16)
    proj_out = lax.psum(part_sum, 'a').astype(jnp.float32)
    hidden = (hidden.astype(jnp.float32) + rms_norm(proj_out, post_gain)).astype(jnp.bfloat16)
    return hidden, out_k, out_v


def solution(mesh):
    cache_in = P('dp', None, 'a', None)
    cache_out = P('dp', 'a', None, None)
    rows_spec = P('dp', None)
    layer_specs = (P(None, 'a'), P(None, 'a'), P(None, 'a'), P('a', None), P(None), P(None))
    in_specs = (rows_spec, cache_in, cache_in, cache_in, cache_in) + layer_specs + layer_specs
    out_specs = (rows_spec, cache_out, cache_out, cache_out, cache_out)

    def device_step(hidden_in, loc_k, loc_v, glo_k, glo_v, loc_wq, loc_wk, loc_wv, loc_wo, loc_pre, loc_post, glo_wq, glo_wk, glo_wv, glo_wo, glo_pre, glo_post):
        loc_k, loc_v, glo_k, glo_v = [lax.all_to_all(kv_cache, 'a', 1, 2, tiled=True) for kv_cache in (loc_k, loc_v, glo_k, glo_v)]
        hidden, loc_k_out, loc_v_out = decode_layer(hidden_in, loc_k, loc_v, loc_wq, loc_wk, loc_wv, loc_wo, loc_pre, loc_post, True)
        hidden_out, glo_k_out, glo_v_out = decode_layer(hidden, glo_k, glo_v, glo_wq, glo_wk, glo_wv, glo_wo, glo_pre, glo_post, False)
        return hidden_out, loc_k_out, loc_v_out, glo_k_out, glo_v_out

    return jax.shard_map(device_step, mesh=mesh, in_specs=in_specs, out_specs=out_specs, check_vma=False)
```

profile of v0, /device:TPU:0, one launch (start us, length us, event | category | flops | bytes accessed | tf_op | source)
XLA Modules:
  0.0 1499.0 jit_solution(7013931670630644989)
XLA Ops:
  0.6 20.8 %copy.65 = bf16[8,4,1536,256]{3,2,0,1:T(8,128)(2,1)} copy(bf16[8,4,1536,256]{3,2,1,0:T(8,128)(2,1)} %param.18) | data formatting | bytes 50331648 | tf_op args[1]
  21.4 8.4 all-to-all-start
  29.8 20.5 %copy.67 = bf16[8,4,1536,256]{3,2,0,1:T(8,128)(2,1)} copy(bf16[8,4,1536,256]{3,2,1,0:T(8,128)(2,1)} %param.19) | data formatting | bytes 50331648 | tf_op args[2]
  50.3 253.1 %all-to-all-done = bf16[8,4,1536,256]{3,2,0,1:T(8,128)(2,1)} async-done(((bf16[8,4,1536,256]{3,2,0,1:T(8,128)(2,1)}), bf16[8,4,1536,256]{3,2,0,1:T(8,128)(2,1)}, u32[]{:S(2)}, u32[]{:S(2)}) %all-to-all-start) | async-done | bytes 25165856 | tf_op jit(solution)/shard_map/all_to_all | solution.py:84
  303.4 8.5 all-to-all-start.1
  311.9 20.5 %copy.69 = bf16[8,4,1536,256]{3,2,0,1:T(8,128)(2,1)} copy(bf16[8,4,1536,256]{3,2,1,0:T(8,128)(2,1)} %param.20) | data formatting | bytes 50331648 | tf_op args[3]
  332.4 252.1 %all-to-all-done.1 = bf16[8,4,1536,256]{3,2,0,1:T(8,128)(2,1)} async-done(((bf16[8,4,1536,256]{3,2,0,1:T(8,128)(2,1)}), bf16[8,4,1536,256]{3,2,0,1:T(8,128)(2,1)}, u32[]{:S(2)}, u32[]{:S(2)}) %all-to-all-start.1) | async-done | bytes 25165856 | tf_op jit(solution)/shard_map/all_to_all | solution.py:84
  584.5 8.5 all-to-all-start.2
  593.0 20.5 %copy.71 = bf16[8,4,1536,256]{3,2,0,1:T(8,128)(2,1)} copy(bf16[8,4,1536,256]{3,2,1,0:T(8,128)(2,1)} %param.21) | data formatting | bytes 50331648 | tf_op args[4]
  613.5 252.0 %all-to-all-done.2 = bf16[8,4,1536,256]{3,2,0,1:T(8,128)(2,1)} async-done(((bf16[8,4,1536,256]{3,2,0,1:T(8,128)(2,1)}), bf16[8,4,1536,256]{3,2,0,1:T(8,128)(2,1)}, u32[]{:S(2)}, u32[]{:S(2)}) %all-to-all-start.2) | async-done | bytes 25165856 | tf_op jit(solution)/shard_map/all_to_all | solution.py:84
  865.6 8.5 all-to-all-start.3
  879.4 2.2 fusion.74
  881.8 20.5 %copy.66 = bf16[8,4,1536,256]{3,2,1,0:T(8,128)(2,1)} copy(bf16[8,4,1536,256]{3,2,0,1:T(8,128)(2,1)} %all-to-all-done) | data formatting | bytes 50331648 | tf_op jit(solution)/shard_map/all_to_all | solution.py:84
  902.4 8.6 slice.72
  911.0 14.9 slice.64
  925.9 20.5 %copy.68 = bf16[8,4,1536,256]{3,2,1,0:T(8,128)(2,1)} copy(bf16[8,4,1536,256]{3,2,0,1:T(8,128)(2,1)} %all-to-all-done.1) | data formatting | bytes 50331648 | tf_op jit(solution)/shard_map/all_to_all | solution.py:84
  946.4 8.7 slice.73
  955.2 15.0 %slice.67 = bf16[8,1,4095,256]{3,2,0,1:T(8,128)(2,1)} slice(bf16[8,1,6144,256]{3,2,0,1:T(8,128)(2,1)} %bitcast.88), slice={[0:8], [0:1], [2049:6144], [0:256]} | slice | bytes 33546240 | tf_op jit(solution)/shard_map/slice | solution.py:57
  970.2 10.4 fusion.80
  980.9 8.1 fusion.31
  989.5 163.3 %psum.14 = bf16[8,2560]{1,0:T(8,128)(2,1)S(1)} all-reduce(bf16[8,2560]{1,0:T(8,128)(2,1)S(1)} %convolution_convert_fusion.1), channel_id=1, replica_groups=mesh['dp'=2,'a'=4] {'a'}, use_global_device_ids=true, to_apply=%region_3.4 | all-reduce | flops 20480 | bytes 81920 | tf_op jit(solution)/shard_map/psum | solution.py:70
  1153.1 1.6 convolution_bitcast_fusion
  1154.8 2.2 fusion.70
  1158.7 20.5 %copy.70 = bf16[8,4,1536,256]{3,2,1,0:T(8,128)(2,1)} copy(bf16[8,4,1536,256]{3,2,0,1:T(8,128)(2,1)} %all-to-all-done.2) | data formatting | bytes 50331648 | tf_op jit(solution)/shard_map/all_to_all | solution.py:84
  1179.4 11.6 fusion.82
  1191.4 20.5 %copy.72 = bf16[8,4,1536,256]{3,2,1,0:T(8,128)(2,1)} copy(bf16[8,4,1536,256]{3,2,0,1:T(8,128)(2,1)} %all-to-all-done.3) | data formatting | bytes 50331648 | tf_op jit(solution)/shard_map/all_to_all | solution.py:84
  1211.9 10.1 fusion.21
  1222.5 10.6 psum.15
  1235.4 116.6 %concatenate.116 = bf16[8,1,6656,256]{3,2,0,1:T(8,128)(2,1)} concatenate(bf16[8,1,6144,256]{3,2,0,1:T(8,128)(2,1)} %bitcast.86, bf16[8,1,1,256]{3,2,0,1:T(2,128)(2,1)S(1)} %copy.79, bf16[8,1,511,256]{3,2,0,1:T(8,128)(2,1)} %broadcast_in_dim.2), dimensions={2} | concatenate | bytes 54525952 | tf_op jit(solution)/shard_map/concatenate | solution.py:66
  1352.1 116.7 %concatenate.115 = bf16[8,1,6656,256]{3,2,0,1:T(8,128)(2,1)} concatenate(bf16[8,1,6144,256]{3,2,0,1:T(8,128)(2,1)} %bitcast.84, bf16[8,1,1,256]{3,2,0,1:T(2,128)(2,1)S(1)} %copy.77, bf16[8,1,511,256]{3,2,0,1:T(8,128)(2,1)} %broadcast_in_dim.2), dimensions={2} | concatenate | bytes 54525952 | tf_op jit(solution)/shard_map/concatenate | solution.py:65
  1468.7 15.1 %fusion.1 = bf16[8,1,4096,256]{3,2,1,0:T(8,128)(2,1)} fusion(bf16[8,1,1,256]{3,2,0,1:T(2,128)(2,1)S(1)} %copy-done.3, bf16[8,1,4095,256]{3,2,0,1:T(8,128)(2,1)} %slice.67, bf16[8,1,2047,256]{3,2,0,1:T(8,128)(2,1)} %slice.73), kind=kLoop, calls=%fused_computation.2 | loop fusion | flops 50331648 | bytes 41938944
  1483.9 15.2 %fusion.3 = bf16[8,1,4096,256]{3,2,1,0:T(8,128)(2,1)} fusion(bf16[8,1,4095,256]{3,2,0,1:T(8,128)(2,1)} %slice.64, bf16[8,1,1,128]{3,2,0,1:T(2,128)(2,1)S(1)} %copy-done.4, bf16[8,1,1,128]{3,2,0,1:T(2,128)(2,1)S(1)} %copy-done.5, bf16[8,1,2047,256]{3,2,0,1:T(8,128)(2,1)} %slice.72), kind=kLoop, calls=%fused_computation.5 | loop fusion | flops 67108864 | bytes 41938944
  (65 shorter events, 11.7 us)
Async XLA Ops:
  0.6 988.4 %copy-start = (bf16[512,2560]{1,0:T(8,128)(2,1)S(1)}, bf16[512,2560]{1,0:T(8,128)(2,1)}, u32[]{:S(2)}) copy-start(bf16[512,2560]{1,0:T(8,128)(2,1)} %param.25) | copy-start | bytes 7864324
  21.4 282.0 %all-to-all-start = ((bf16[8,4,1536,256]{3,2,0,1:T(8,128)(2,1)}), bf16[8,4,1536,256]{3,2,0,1:T(8,128)(2,1)}, u32[]{:S(2)}, u32[]{:S(2)}) async-start(bf16[8,4,1536,256]{3,2,0,1:T(8,128)(2,1)} %copy.65), calls=%async_computation | async-start | bytes 50331648 | tf_op jit(solution)/shard_map/all_to_all | solution.py:84
  303.4 281.1 %all-to-all-start.1 = ((bf16[8,4,1536,256]{3,2,0,1:T(8,128)(2,1)}), bf16[8,4,1536,256]{3,2,0,1:T(8,128)(2,1)}, u32[]{:S(2)}, u32[]{:S(2)}) async-start(bf16[8,4,1536,256]{3,2,0,1:T(8,128)(2,1)} %copy.67), calls=%async_computation.1 | async-start | bytes 50331648 | tf_op jit(solution)/shard_map/all_to_all | solution.py:84
  584.5 281.1 %all-to-all-start.2 = ((bf16[8,4,1536,256]{3,2,0,1:T(8,128)(2,1)}), bf16[8,4,1536,256]{3,2,0,1:T(8,128)(2,1)}, u32[]{:S(2)}, u32[]{:S(2)}) async-start(bf16[8,4,1536,256]{3,2,0,1:T(8,128)(2,1)} %copy.69), calls=%async_computation.2 | async-start | bytes 50331648 | tf_op jit(solution)/shard_map/all_to_all | solution.py:84
  613.5 260.7 %copy-start.2 = (bf16[8,2560]{1,0:T(8,128)(2,1)S(1)}, bf16[8,2560]{1,0:T(8,128)(2,1)}, u32[]{:S(2)}) copy-start(bf16[8,2560]{1,0:T(8,128)(2,1)} %param.17) | copy-start | bytes 122884
  613.5 260.8 %copy-start.6 = (bf16[2560]{0:T(1024)(128)(2,1)S(1)}, bf16[2560]{0:T(1024)(128)(2,1)}, u32[]{:S(2)}) copy-start(bf16[2560]{0:T(1024)(128)(2,1)} %param.26) | copy-start | bytes 15364
  613.5 268.3 %copy-start.7 = (bf16[2560]{0:T(1024)(128)(2,1)S(1)}, bf16[2560]{0:T(1024)(128)(2,1)}, u32[]{:S(2)}) copy-start(bf16[2560]{0:T(1024)(128)(2,1)} %param.32) | copy-start | bytes 15364
  613.5 268.3 %copy-start.8 = (bf16[2560]{0:T(1024)(128)(2,1)S(1)}, bf16[2560]{0:T(1024)(128)(2,1)}, u32[]{:S(2)}) copy-start(bf16[2560]{0:T(1024)(128)(2,1)} %param.27) | copy-start | bytes 15364
  613.5 268.3 %copy-start.9 = (bf16[2560]{0:T(1024)(128)(2,1)S(1)}, bf16[2560]{0:T(1024)(128)(2,1)}, u32[]{:S(2)}) copy-start(bf16[2560]{0:T(1024)(128)(2,1)} %param.33) | copy-start | bytes 15364
  865.6 325.8 %all-to-all-start.3 = ((bf16[8,4,1536,256]{3,2,0,1:T(8,128)(2,1)}), bf16[8,4,1536,256]{3,2,0,1:T(8,128)(2,1)}, u32[]{:S(2)}, u32[]{:S(2)}) async-start(bf16[8,4,1536,256]{3,2,0,1:T(8,128)(2,1)} %copy.71), calls=%async_computation.3 | async-start | bytes 50331648 | tf_op jit(solution)/shard_map/all_to_all | solution.py:84
  1211.9 10.2 copy-start.1
  1352.1 116.7 %copy-start.3 = (bf16[8,1,1,256]{3,2,0,1:T(2,128)(2,1)S(1)}, bf16[8,1,1,256]{3,2,0,1:T(2,128)(2,1)}, u32[]{:S(2)}) copy-start(bf16[8,1,1,256]{3,2,0,1:T(2,128)(2,1)} %copy.75) | copy-start | bytes 12292
  1468.7 15.1 %copy-start.4 = (bf16[8,1,1,128]{3,2,0,1:T(2,128)(2,1)S(1)}, bf16[8,1,1,128]{3,2,0,1:T(2,128)(2,1)}, u32[]{:S(2)}) copy-start(bf16[8,1,1,128]{3,2,0,1:T(2,128)(2,1)} %copy.74) | copy-start | bytes 6148
  1468.7 15.1 %copy-start.5 = (bf16[8,1,1,128]{3,2,0,1:T(2,128)(2,1)S(1)}, bf16[8,1,1,128]{3,2,0,1:T(2,128)(2,1)}, u32[]{:S(2)}) copy-start(bf16[8,1,1,128]{3,2,0,1:T(2,128)(2,1)} %copy.73) | copy-start | bytes 6148
where the time goes:
time: 1510 us; the launch traced here: 1500 us
  waiting for transfers between devices  757 us (50%)
  local copies, waits for them, and re-layouts  448 us (30%)
  blocking collectives  174 us (12%)
  matrix products  52.3 us (3%)
  starting transfers between devices  33.9 us (2%)
  other arithmetic  32.6 us (2%)
    all_to_all x4, waiting for transfers between devices, device_step(): lax.all_to_all(kv_cache, 'a', 1, 2, tiled=True)  757 us
    psum x2, blocking collectives, decode_layer(): proj_out = lax.psum(part_sum, 'a').astype(jnp.float32)  174 us
    concatenate x1, local copies, waits for them, and re-layouts, decode_layer(): out_k = jnp.concatenate([cache_k, new_k[:, :, None], zero_pad], axis=2)  117 us
    concatenate x1, local copies, waits for them, and re-layouts, decode_layer(): out_v = jnp.concatenate([cache_v, new_v[:, :, None], zero_pad], axis=2)  117 us
    unnamed x26, local copies, waits for them, and re-layouts  82.4 us
    all_to_all x4, local copies, waits for them, and re-layouts, device_step(): lax.all_to_all(kv_cache, 'a', 1, 2, tiled=True)  82.1 us
    all_to_all x4, starting transfers between devices, device_step(): lax.all_to_all(kv_cache, 'a', 1, 2, tiled=True)  33.9 us
    unnamed x2, other arithmetic  30.3 us
  transfers between devices with their start and end apart: 4, of which 3 were waited for; matrix products, arithmetic and copies ran while one was open for 14% of the time, Pallas kernels for 0%

commit v1 on v0

v1 whole, which is shorter than its diff:
```python
import jax
import jax.numpy as jnp
import numpy as np
from jax import lax
from jax.experimental import pallas as pl
from jax.experimental.pallas import tpu as pltpu
from jax.sharding import PartitionSpec as P

SOFTCAP = 50.0
NORM_EPS = 1e-6
ROPE_BASE = 10000.0
WINDOW = 4096
CACHE_ROOM = 512

GROUP = 4
ROWS = 8
BLOCK = 1536
UNIT = 512
HEAD = 256
SEQ = GROUP * BLOCK
PER = BLOCK // UNIT
GLO_UNITS = SEQ // UNIT
LOC_UNITS = WINDOW // UNIT
FIRST_UNIT = (SEQ - WINDOW) // UNIT
STEPS = 4 * ROWS * PER
DEPTH = 2
LEFT = 0
MESH = pl.DeviceIdType.MESH
LOW = -1e30


def peers(me):
    return (me + 1 - 2 * (me % 2), (me + 2) % 4, 3 - me)


def norm(hidden, gain):
    mean_sq = jnp.mean(hidden * hidden, axis=-1, keepdims=True)
    return hidden * lax.rsqrt(mean_sq + NORM_EPS) * (1.0 + gain.astype(jnp.float32))


def softcap(scores):
    return SOFTCAP * jnp.tanh(scores * (HEAD ** -0.5) / SOFTCAP)


def move_kernel(hid, trig, lpre, lpost, gpre, gpost, lk, lv, gk, gv, lwq, lwk, lwv, lwo, gwq, gwk, gwv, gwo,
                land_lk, land_lv, land_gk, land_gv, hid_out, new_kv,
                wq, wk, wv, wo, kvbuf, qbuf, part, precv, ybuf,
                bulk_send, loc_recv, glo_recv, w_sem, kv_sem, ex_send, ex_recv):
    dp = lax.axis_index("dp")
    me = lax.axis_index("a")
    dest = peers(me)
    caches = (lk, lv, gk, gv)
    lands = (land_lk, land_lv, land_gk, land_gv)

    barrier = pltpu.get_barrier_semaphore()
    for peer in dest:
        pl.semaphore_signal(barrier, inc=1, device_id=(dp, peer), device_id_type=MESH)
    pl.semaphore_wait(barrier, 3)

    def valid(step, k):
        c, r, j = step // (ROWS * PER), (step // PER) % ROWS, step % PER
        in_window = jnp.logical_or(c >= 2, PER * me + j >= FIRST_UNIT)
        ok = jnp.logical_and(step >= 0, in_window)
        if k == 1 and LEFT:
            later = jnp.logical_and(jnp.logical_and(c == 3, r >= ROWS - LEFT), me >= 2)
            ok = jnp.logical_and(ok, jnp.logical_not(later))
        return ok

    def pump(step):
        c, r, j = step // (ROWS * PER), (step // PER) % ROWS, step % PER
        slot = step % DEPTH
        for k in range(3):
            @pl.when(valid(step - DEPTH, k))
            def _():
                pltpu.make_async_remote_copy(
                    src_ref=gk.at[0, 0, pl.ds(0, UNIT)], dst_ref=land_gk.at[0, 0, pl.ds(0, UNIT)],
                    send_sem=bulk_send.at[k, slot], recv_sem=glo_recv.at[0, 0],
                    device_id=(dp, dest[k]), device_id_type=MESH).wait_send()
        unit = PER * me + j
        for i in range(4):
            place = unit % LOC_UNITS if i < 2 else unit
            sem = loc_recv.at[i, place] if i < 2 else glo_recv.at[i - 2, place]
            for k in range(3):
                @pl.when(jnp.logical_and(c == i, valid(step, k)))
                def _():
                    pltpu.make_async_remote_copy(
                        src_ref=caches[i].at[r, dest[k], pl.ds(pl.multiple_of(j * UNIT, UNIT), UNIT)],
                        dst_ref=lands[i].at[r, 0, pl.ds(pl.multiple_of(place * UNIT, UNIT), UNIT)],
                        send_sem=bulk_send.at[k, slot], recv_sem=sem,
                        device_id=(dp, dest[k]), device_id_type=MESH).start()

    def exchange(index, src_of, dst):
        copies = []
        for k in range(3):
            copies.append(pltpu.make_async_remote_copy(
                src_ref=src_of(dest[k]), dst_ref=dst.at[me], send_sem=ex_send.at[index, k], recv_sem=ex_recv.at[index, k],
                device_id=(dp, dest[k]), device_id_type=MESH))
        for copy in copies:
            copy.start()
        return copies

    def finish(copies):
        for copy in copies:
            copy.wait()

    weights = [pltpu.make_async_copy(src, dst, w_sem.at[i]) for i, (src, dst) in enumerate((
        (lwq, wq.at[0]), (lwk, wk.at[0]), (lwv, wv.at[0]), (lwo, wo.at[0]),
        (gwq, wq.at[1]), (gwk, wk.at[1]), (gwv, wv.at[1]), (gwo, wo.at[1])))]

    pump(0)
    for copy in weights:
        copy.start()
    pump(1)

    cosine, sine = trig[0:1, :], trig[1:2, :]

    def rope(heads):
        first, second = heads[:, :HEAD // 2], heads[:, HEAD // 2:]
        return jnp.concatenate([first * cosine - second * sine, second * cosine + first * sine], axis=-1)

    def layer(index, hidden, key_ref, value_ref, pre, post, step):
        normed = norm(hidden, pre[...]).astype(jnp.bfloat16)
        if index == 0:
            for copy in weights[:4]:
                copy.wait()
        else:
            for copy in weights[4:]:
                copy.wait()
        q = jnp.dot(normed, wq[index], preferred_element_type=jnp.float32)
        q = jnp.concatenate([rope(q[:, :HEAD]), rope(q[:, HEAD:])], axis=0).astype(jnp.bfloat16)
        new_k = rope(jnp.dot(normed, wk[index], preferred_element_type=jnp.float32)).astype(jnp.bfloat16)
        new_v = jnp.dot(normed, wv[index], preferred_element_type=jnp.float32).astype(jnp.bfloat16)
        new_kv[2 * index] = new_k
        new_kv[2 * index + 1] = new_v
        own_q = qbuf.at[index]
        own_q[me] = q
        sent = exchange(3 * index, lambda peer: own_q.at[me], own_q)
        pump(step)
        finish(sent)

        def fetch(item, slot):
            h, r = item // ROWS, item % ROWS
            return (pltpu.make_async_copy(key_ref.at[r, h], kvbuf.at[slot, 0], kv_sem.at[slot, 0]),
                    pltpu.make_async_copy(value_ref.at[r, h], kvbuf.at[slot, 1], kv_sem.at[slot, 1]))

        for copy in fetch(0, 0):
            copy.start()
        items = GROUP * ROWS

        def body(item, carry):
            pump(step + 1 + item)
            slot = item % 2
            h, r = item // ROWS, item % ROWS

            @pl.when(item + 1 < items)
            def _():
                for copy in fetch(item + 1, 1 - slot):
                    copy.start()

            copy_k, copy_v = fetch(item, slot)
            copy_k.wait()
            scores = softcap(lax.dot_general(own_q[h], kvbuf[slot, 0], (((1,), (1,)), ((), ())),
                                             preferred_element_type=jnp.float32))
            if index == 0:
                place = me * BLOCK + lax.broadcasted_iota(jnp.int32, scores.shape, 1)
                inside = place > SEQ - WINDOW
                scores = jnp.where(inside, scores, LOW)
            top = jnp.max(scores, axis=-1, keepdims=True)
            e = jnp.exp(scores - top)
            if index == 0:
                e = jnp.where(inside, e, 0.0)
            total = jnp.sum(e, axis=-1, keepdims=True)
            copy_v.wait()
            out = jnp.dot(e.astype(jnp.bfloat16), kvbuf[slot, 1], preferred_element_type=jnp.float32)
            wide = jnp.concatenate([out, jnp.broadcast_to(top, (2 * ROWS, 128)),
                                    jnp.broadcast_to(total, (2 * ROWS, 128))], axis=-1)
            row = lax.broadcasted_iota(jnp.int32, wide.shape, 0) % ROWS
            part[index, h] = jnp.where(row == r, wide, part[index, h])
            return carry

        lax.fori_loop(0, items, body, 0)
        step = step + 1 + items

        sent = exchange(3 * index + 1, lambda peer: part.at[index, peer], precv.at[index])
        precv[index, me] = part[index, me]
        pump(step)
        new_k2 = jnp.concatenate([new_k, new_k], axis=0).astype(jnp.float32)
        new_v2 = jnp.concatenate([new_v, new_v], axis=0).astype(jnp.float32)
        new_s = softcap(jnp.sum(q.astype(jnp.float32) * new_k2, axis=-1, keepdims=True))
        finish(sent)
        top = new_s
        for d in range(GROUP):
            top = jnp.maximum(top, precv[index, d, :, HEAD:HEAD + 1])
        new_e = jnp.exp(new_s - top)
        total = new_e
        acc = new_e.astype(jnp.bfloat16).astype(jnp.float32) * new_v2
        for d in range(GROUP):
            scale = jnp.exp(precv[index, d, :, HEAD:HEAD + 1] - top)
            total = total + scale * precv[index, d, :, HEAD + 128:HEAD + 129]
            acc = acc + scale * precv[index, d, :, :HEAD]
        att = (acc / total).astype(jnp.bfloat16)
        own = jnp.concatenate([att[:ROWS], att[ROWS:]], axis=-1)
        y = jnp.dot(own, wo[index], preferred_element_type=jnp.float32).astype(jnp.bfloat16)
        y_ref = ybuf.at[index]
        y_ref[me] = y
        sent = exchange(3 * index + 2, lambda peer: y_ref.at[me], y_ref)
        pump(step + 1)
        finish(sent)
        summed = y_ref[0].astype(jnp.float32)
        for d in range(1, GROUP):
            summed = summed + y_ref[d].astype(jnp.float32)
        return (hidden + norm(summed, post[...])).astype(jnp.bfloat16), step + 2

    part[...] = jnp.zeros_like(part)
    hidden, step = layer(0, hid[...].astype(jnp.float32), lk, lv, lpre, lpost, 2)
    hidden, step = layer(1, hidden.astype(jnp.float32), gk, gv, gpre, gpost, step)
    hid_out[...] = hidden

    def rest(s, carry):
        pump(s)
        return carry

    lax.fori_loop(step, STEPS, rest, 0)

    for s in range(STEPS - DEPTH, STEPS):
        for k in range(3):
            @pl.when(valid(s, k))
            def _():
                pltpu.make_async_remote_copy(
                    src_ref=gk.at[0, 0, pl.ds(0, UNIT)], dst_ref=land_gk.at[0, 0, pl.ds(0, UNIT)],
                    send_sem=bulk_send.at[k, s % DEPTH], recv_sem=glo_recv.at[0, 0],
                    device_id=(dp, dest[k]), device_id_type=MESH).wait_send()
    for i in range(4):
        for u in range(LOC_UNITS if i < 2 else GLO_UNITS):
            owner = (u if i >= 2 or u >= FIRST_UNIT else u + LOC_UNITS) // PER
            sem = loc_recv.at[i, u] if i < 2 else glo_recv.at[i - 2, u]

            def await_rows(rows):
                view = lands[i].at[pl.ds(0, rows), :, pl.ds(u * UNIT, UNIT)]
                pltpu.make_async_remote_copy(
                    src_ref=view, dst_ref=view, send_sem=bulk_send.at[0, 0], recv_sem=sem,
                    device_id=(dp, dest[0]), device_id_type=MESH).wait_recv()

            if LEFT and i == 3 and owner >= 2:
                short = me == owner - 2

                @pl.when(short)
                def _():
                    await_rows(ROWS - LEFT)

                @pl.when(jnp.logical_and(me != owner, jnp.logical_not(short)))
                def _():
                    await_rows(ROWS)
            else:
                @pl.when(me != owner)
                def _():
                    await_rows(ROWS)


SLOTS = 6


def write_kernel(hid, new_kv, lk, lv, gk, gv, land_lk, land_lv, land_gk, land_gv,
                 hid_out, lk_out, lv_out, gk_out, gv_out, buf, in_sem, out_sem):
    me = lax.axis_index("a")
    hid_out[...] = hid[...]
    jobs = []
    for i in range(4):
        for u in range(LOC_UNITS if i < 2 else GLO_UNITS + 1):
            jobs.append((i, u))
    caches = (lk, lv, gk, gv)
    lands = (land_lk, land_lv, land_gk, land_gv)
    outs = (lk_out, lv_out, gk_out, gv_out)

    def load(n):
        i, u = jobs[n]
        slot = n % SLOTS
        if i >= 2 and u == GLO_UNITS:
            return
        full = u if i >= 2 or u >= FIRST_UNIT else u + LOC_UNITS
        owner, j = full // PER, full % PER

        @pl.when(me == owner)
        def _():
            pltpu.make_async_copy(caches[i].at[:, owner, pl.ds(j * UNIT, UNIT)], buf.at[slot], in_sem.at[slot]).start()

        @pl.when(me != owner)
        def _():
            pltpu.make_async_copy(lands[i].at[:, 0, pl.ds(u * UNIT, UNIT)], buf.at[slot], in_sem.at[slot]).start()

    def store(n):
        i, u = jobs[n]
        slot = n % SLOTS
        return pltpu.make_async_copy(buf.at[slot], outs[i].at[:, 0, pl.ds(u * UNIT, UNIT)], out_sem.at[slot])

    ahead = SLOTS // 2
    for n in range(ahead):
        load(n)
    for n, (i, u) in enumerate(jobs):
        slot = n % SLOTS
        if n + ahead < len(jobs):
            if n + ahead >= SLOTS:
                store(n + ahead - SLOTS).wait()
            load(n + ahead)
        pad = i >= 2 and u == GLO_UNITS
        if not pad:
            pltpu.make_async_copy(lands[i].at[:, 0, pl.ds(0, UNIT)], buf.at[slot], in_sem.at[slot]).wait()
        else:
            buf[slot] = jnp.zeros((ROWS, UNIT, HEAD), jnp.bfloat16)
        if pad or (i < 2 and u == SEQ % WINDOW // UNIT):
            head = buf[slot, :, 0:16, :].astype(jnp.float32)
            first = lax.broadcasted_iota(jnp.int32, head.shape, 1) == 0
            new = jnp.broadcast_to(new_kv[i].astype(jnp.float32)[:, None, :], head.shape)
            buf[slot, :, 0:16, :] = jnp.where(first, new, head).astype(jnp.bfloat16)
        store(n).start()
    for n in range(len(jobs) - SLOTS, len(jobs)):
        store(n).wait()


def trig_table():
    half = HEAD // 2
    inv_freq = ROPE_BASE ** (-2.0 * np.arange(half) / HEAD)
    angles = SEQ * inv_freq
    return np.stack([np.cos(angles), np.sin(angles)]).astype(np.float32)


def solution(mesh):
    cache_in = P('dp', None, 'a', None)
    cache_out = P('dp', 'a', None, None)
    rows_spec = P('dp', None)
    layer_specs = (P(None, 'a'), P(None, 'a'), P(None, 'a'), P('a', None), P(None), P(None))
    in_specs = (rows_spec, cache_in, cache_in, cache_in, cache_in) + layer_specs + layer_specs
    out_specs = (rows_spec, cache_out, cache_out, cache_out, cache_out)
    bf16, f32 = jnp.bfloat16, jnp.float32
    anywhere = pl.BlockSpec(memory_space=pl.ANY)
    vmem = pl.BlockSpec(memory_space=pltpu.VMEM)

    def device_step(hidden_in, loc_k, loc_v, glo_k, glo_v, loc_wq, loc_wk, loc_wv, loc_wo, loc_pre, loc_post, glo_wq, glo_wk, glo_wv, glo_wo, glo_pre, glo_post):
        model = hidden_in.shape[1]
        gains = [g.reshape(1, model) for g in (loc_pre, loc_post, glo_pre, glo_post)]
        loc_land = jax.ShapeDtypeStruct((ROWS, 1, WINDOW, HEAD), bf16)
        glo_land = jax.ShapeDtypeStruct((ROWS, 1, SEQ, HEAD), bf16)
        dma = pltpu.SemaphoreType.DMA
        moved = pl.pallas_call(
            move_kernel,
            out_shape=(loc_land, loc_land, glo_land, glo_land,
                       jax.ShapeDtypeStruct((ROWS, model), bf16), jax.ShapeDtypeStruct((4, ROWS, HEAD), bf16)),
            in_specs=[vmem] * 6 + [anywhere] * 12,
            out_specs=(anywhere,) * 4 + (vmem, vmem),
            scratch_shapes=[
                pltpu.VMEM((2,) + loc_wq.shape, bf16), pltpu.VMEM((2,) + loc_wk.shape, bf16),
                pltpu.VMEM((2,) + loc_wv.shape, bf16), pltpu.VMEM((2,) + loc_wo.shape, bf16),
                pltpu.VMEM((2, 2, BLOCK, HEAD), bf16),
                pltpu.VMEM((2, GROUP, 2 * ROWS, HEAD), bf16),
                pltpu.VMEM((2, GROUP, 2 * ROWS, 2 * HEAD), f32),
                pltpu.VMEM((2, GROUP, 2 * ROWS, 2 * HEAD), f32),
                pltpu.VMEM((2, GROUP, ROWS, model), bf16),
                dma((3, DEPTH)), dma((2, LOC_UNITS)), dma((2, GLO_UNITS)), dma((8,)), dma((2, 2)),
                dma((6, 3)), dma((6, 3))],
            compiler_params=pltpu.CompilerParams(collective_id=0, has_side_effects=True),
        )(hidden_in, jnp.asarray(trig_table()), *gains, loc_k, loc_v, glo_k, glo_v,
          loc_wq, loc_wk, loc_wv, loc_wo, glo_wq, glo_wk, glo_wv, glo_wo)
        land, hid, new_kv = moved[:4], moved[4], moved[5]
        return pl.pallas_call(
            write_kernel,
            out_shape=(jax.ShapeDtypeStruct((ROWS, model), bf16),)
            + (jax.ShapeDtypeStruct((ROWS, 1, WINDOW, HEAD), bf16),) * 2
            + (jax.ShapeDtypeStruct((ROWS, 1, SEQ + CACHE_ROOM, HEAD), bf16),) * 2,
            in_specs=[vmem, vmem] + [anywhere] * 8,
            out_specs=(vmem,) + (anywhere,) * 4,
            scratch_shapes=[pltpu.VMEM((SLOTS, ROWS, UNIT, HEAD), bf16), dma((SLOTS,)), dma((SLOTS,))],
            cost_estimate=pl.CostEstimate(flops=10 ** 9, bytes_accessed=180 * 10 ** 6, transcendentals=0),
        )(hid, new_kv, loc_k, loc_v, glo_k, glo_v, *land)

    return jax.shard_map(device_step, mesh=mesh, in_specs=in_specs, out_specs=out_specs, check_vma=False)
```

time: 1510 us -> 1160 us (0.77)
  Pallas kernels: 0 us -> 1150 us
  waiting for transfers between devices: 757 us -> 0 us
  local copies, waits for them, and re-layouts: 448 us -> 5.19 us
  blocking collectives: 174 us -> 0 us
  matrix products: 52.3 us -> 0 us
  starting transfers between devices: 33.9 us -> 0 us
  other arithmetic: 32.6 us -> 0 us
    pallas_call x0 -> x2, Pallas kernels: none -> 1150 us  [the longest x1 1090 us: device_step(): pl.pallas_call(move_kernel, out_shape=(loc_land, loc_land, glo_land, glo_...]
    all_to_all x4 -> x0, waiting for transfers between devices: 757 us -> none  [device_step(): lax.all_to_all(kv_cache, 'a', 1, 2, tiled=True)]
    concatenate x5 -> x0, local copies, waits for them, and re-layouts: 235 us -> none  [the longest x1 117 us: decode_layer(): out_k = jnp.concatenate([cache_k, new_k[:, :, None], zero_pad], axis=2)]
    psum x2 -> x0, blocking collectives: 174 us -> none  [decode_layer(): proj_out = lax.psum(part_sum, 'a').astype(jnp.float32)]
    unnamed x26 -> x0, local copies, waits for them, and re-layouts: 82.4 us -> none
    all_to_all x4 -> x0, local copies, waits for them, and re-layouts: 82.1 us -> none  [device_step(): lax.all_to_all(kv_cache, 'a', 1, 2, tiled=True)]
    dot_general x14 -> x0, matrix products: 52.3 us -> none  [the longest x2 22 us: attend(): jnp.einsum('bkgd,bkld->bkgl', q_heads, old_k, preferred_element_type=jnp....]
    slice x5 -> x0, local copies, waits for them, and re-layouts: 47.3 us -> none  [the longest x1 15 us: decode_layer(): old_v = cache_v[:, :, seq_len - WINDOW + 1:]]
  transfers between devices with their start and end apart: 4 -> 0, of which waited for: 3 -> 0; matrix products, arithmetic and copies ran while one was open for 14% -> 0% of each run, Pallas kernels for 0% -> 0%
where the time goes in v1:
time: 1160 us
  Pallas kernels  1150 us (99%)
    pallas_call x1, Pallas kernels, device_step(): pl.pallas_call(move_kernel, out_shape=(loc_land, loc_land, glo_land, glo_...  1090 us
    pallas_call x1, Pallas kernels, device_step(): pl.pallas_call(write_kernel, out_shape=(jax.ShapeDtypeStruct((ROWS, model...  57.5 us

profile of v1, /device:TPU:0, one launch (start us, length us, event | category | flops | bytes accessed | tf_op | source)
XLA Modules:
  0.0 1155.7 jit_solution(10825426798023147312)
XLA Ops:
  0.6 1.3 reshape.22.lpre
  1.9 1.3 reshape.23.lpost
  3.2 1.3 reshape.24.gpre
  4.5 1.3 reshape.25.gpost
  5.8 1092.4 %shard_map.209 = (bf16[8,1,4096,256]{3,2,1,0:T(8,128)(2,1)}, bf16[8,1,4096,256]{3,2,1,0:T(8,128)(2,1)}, bf16[8,1,6144,256]{3,2,1,0:T(8,128)(2,1)}, bf16[8,1,6144...) custom-call(bf16[8,2560]{1,0:T(8,128)(2,1)} %hid.1, f32[2,128]{1,0:T(2,128)} %constant.2.clone.trig, ...), custom_call_target="tpu_custom_call" | custom-call | tf_op jit(solution)/shard_map/pallas_call | solution.py:344
  1098.2 57.5 %shard_map.210 = (bf16[8,2560]{1,0:T(8,128)(2,1)}, bf16[8,1,4096,256]{3,2,1,0:T(8,128)(2,1)}, bf16[8,1,4096,256]{3,2,1,0:T(8,128)(2,1)}, bf16[8,1,6656,256]{3,2,1,0:T(8,128)(2,1)}, bf16[8,1,6656,256]{3,2,1,0:T(8,128)(2,1)}) custom-call(bf16[8,2560]{1,0:T(8,128)(2,1)} %get-tuple-element.11.hid, bf16[4,8,256]{2,1,0:T(8,128)(2,1)} %get-tuple-element.12.new_kv, ...), custom_call_target="tpu_custom_call" | custom-call | flops 1000000000 | bytes 180000000 | tf_op jit(solution)/shard_map/pallas_call | solution.py:364

commit v2 on v1

--- a/solution.py
+++ b/solution.py
@@ -24,7 +24,7 @@
 FIRST_UNIT = (SEQ - WINDOW) // UNIT
 STEPS = 4 * ROWS * PER
 DEPTH = 2
-LEFT = 0
+LEFT = 4
 MESH = pl.DeviceIdType.MESH
 LOW = -1e30
 
@@ -35,7 +35,7 @@
 
 def norm(hidden, gain):
     mean_sq = jnp.mean(hidden * hidden, axis=-1, keepdims=True)
-    return hidden * lax.rsqrt(mean_sq + NORM_EPS) * (1.0 + gain.astype(jnp.float32))
+    return hidden * lax.rsqrt(mean_sq + NORM_EPS) * (1.0 + gain.astype(jnp.float32).reshape(1, -1))
 
 
 def softcap(scores):
@@ -43,9 +43,9 @@
 
 
 def move_kernel(hid, trig, lpre, lpost, gpre, gpost, lk, lv, gk, gv, lwq, lwk, lwv, lwo, gwq, gwk, gwv, gwo,
-                land_lk, land_lv, land_gk, land_gv, hid_out, new_kv,
+                land_lk, land_lv, land_gk, land_gv, hid_out, new_kv, later,
                 wq, wk, wv, wo, kvbuf, qbuf, part, precv, ybuf,
-                bulk_send, loc_recv, glo_recv, w_sem, kv_sem, ex_send, ex_recv):
+                bulk_send, loc_recv, glo_recv, w_sem, kv_sem, ex_send, ex_recv, late_sem):
     dp = lax.axis_index("dp")
     me = lax.axis_index("a")
     dest = peers(me)
@@ -57,17 +57,21 @@
         pl.semaphore_signal(barrier, inc=1, device_id=(dp, peer), device_id_type=MESH)
     pl.semaphore_wait(barrier, 3)
 
+    def coords(step):
+        c = (step // (ROWS * PER) + 2 - 2 * (me // 2)) % 4
+        return c, (step // PER) % ROWS, step % PER
+
     def valid(step, k):
-        c, r, j = step // (ROWS * PER), (step // PER) % ROWS, step % PER
+        c, r, j = coords(step)
         in_window = jnp.logical_or(c >= 2, PER * me + j >= FIRST_UNIT)
         ok = jnp.logical_and(step >= 0, in_window)
         if k == 1 and LEFT:
-            later = jnp.logical_and(jnp.logical_and(c == 3, r >= ROWS - LEFT), me >= 2)
-            ok = jnp.logical_and(ok, jnp.logical_not(later))
+            late = jnp.logical_and(jnp.logical_and(c == 3, r >= ROWS - LEFT), me >= 2)
+            ok = jnp.logical_and(ok, jnp.logical_not(late))
         return ok
 
     def pump(step):
-        c, r, j = step // (ROWS * PER), (step // PER) % ROWS, step % PER
+        c, r, j = coords(step)
         slot = step % DEPTH
         for k in range(3):
             @pl.when(valid(step - DEPTH, k))
@@ -216,6 +220,20 @@
     hidden, step = layer(1, hidden.astype(jnp.float32), gk, gv, gpre, gpost, step)
     hid_out[...] = hidden
 
+    def late_in(r):
+        return pltpu.make_async_copy(gv.at[ROWS - LEFT + r, dest[1]], kvbuf.at[r // 2, r % 2], late_sem.at[0, r])
+
+    def late_out(r):
+        return pltpu.make_async_copy(kvbuf.at[r // 2, r % 2], later.at[r], late_sem.at[1, r])
+
+    for r in range(LEFT):
+        late_in(r).start()
+    for r in range(LEFT):
+        late_in(r).wait()
+        late_out(r).start()
+    for r in range(LEFT):
+        late_out(r).wait()
+
     def rest(s, carry):
         pump(s)
         return carry
@@ -317,6 +335,17 @@
         store(n).wait()
 
 
+def late_kernel(late, old, out, sem):
+    me = lax.axis_index("a")
+
+    @pl.when(me < 2)
+    def _():
+        place = pl.multiple_of((me + 2) * BLOCK, BLOCK)
+        copy = pltpu.make_async_copy(late, out.at[pl.ds(ROWS - LEFT, LEFT), 0, pl.ds(place, BLOCK)], sem)
+        copy.start()
+        copy.wait()
+
+
 def trig_table():
     half = HEAD // 2
     inv_freq = ROPE_BASE ** (-2.0 * np.arange(half) / HEAD)
@@ -337,16 +366,17 @@
 
     def device_step(hidden_in, loc_k, loc_v, glo_k, glo_v, loc_wq, loc_wk, loc_wv, loc_wo, loc_pre, loc_post, glo_wq, glo_wk, glo_wv, glo_wo, glo_pre, glo_post):
         model = hidden_in.shape[1]
-        gains = [g.reshape(1, model) for g in (loc_pre, loc_post, glo_pre, glo_post)]
+        gains = [loc_pre, loc_post, glo_pre, glo_post]
         loc_land = jax.ShapeDtypeStruct((ROWS, 1, WINDOW, HEAD), bf16)
         glo_land = jax.ShapeDtypeStruct((ROWS, 1, SEQ, HEAD), bf16)
         dma = pltpu.SemaphoreType.DMA
         moved = pl.pallas_call(
             move_kernel,
             out_shape=(loc_land, loc_land, glo_land, glo_land,
-                       jax.ShapeDtypeStruct((ROWS, model), bf16), jax.ShapeDtypeStruct((4, ROWS, HEAD), bf16)),
+                       jax.ShapeDtypeStruct((ROWS, model), bf16), jax.ShapeDtypeStruct((4, ROWS, HEAD), bf16),
+                       jax.ShapeDtypeStruct((LEFT, BLOCK, HEAD), bf16)),
             in_specs=[vmem] * 6 + [anywhere] * 12,
-            out_specs=(anywhere,) * 4 + (vmem, vmem),
+            out_specs=(anywhere,) * 4 + (vmem, vmem, anywhere),
             scratch_shapes=[
                 pltpu.VMEM((2,) + loc_wq.shape, bf16), pltpu.VMEM((2,) + loc_wk.shape, bf16),
                 pltpu.VMEM((2,) + loc_wv.shape, bf16), pltpu.VMEM((2,) + loc_wo.shape, bf16),
@@ -356,12 +386,13 @@
                 pltpu.VMEM((2, GROUP, 2 * ROWS, 2 * HEAD), f32),
                 pltpu.VMEM((2, GROUP, ROWS, model), bf16),
                 dma((3, DEPTH)), dma((2, LOC_UNITS)), dma((2, GLO_UNITS)), dma((8,)), dma((2, 2)),
-                dma((6, 3)), dma((6, 3))],
+                dma((6, 3)), dma((6, 3)), dma((2, LEFT))],
             compiler_params=pltpu.CompilerParams(collective_id=0, has_side_effects=True),
         )(hidden_in, jnp.asarray(trig_table()), *gains, loc_k, loc_v, glo_k, glo_v,
           loc_wq, loc_wk, loc_wv, loc_wo, glo_wq, glo_wk, glo_wv, glo_wo)
-        land, hid, new_kv = moved[:4], moved[4], moved[5]
-        return pl.pallas_call(
+        land, hid, new_kv, later = moved[:4], moved[4], moved[5], moved[6]
+        late = lax.ppermute(later, 'a', [(2, 0), (3, 1)])
+        hidden_out, loc_k_out, loc_v_out, glo_k_out, glo_v_out = pl.pallas_call(
             write_kernel,
             out_shape=(jax.ShapeDtypeStruct((ROWS, model), bf16),)
             + (jax.ShapeDtypeStruct((ROWS, 1, WINDOW, HEAD), bf16),) * 2
@@ -371,5 +402,16 @@
             scratch_shapes=[pltpu.VMEM((SLOTS, ROWS, UNIT, HEAD), bf16), dma((SLOTS,)), dma((SLOTS,))],
             cost_estimate=pl.CostEstimate(flops=10 ** 9, bytes_accessed=180 * 10 ** 6, transcendentals=0),
         )(hid, new_kv, loc_k, loc_v, glo_k, glo_v, *land)
+        glo_v_out = pl.pallas_call(
+            late_kernel,
+            out_shape=jax.ShapeDtypeStruct(glo_v_out.shape, bf16),
+            in_specs=[vmem, anywhere],
+            out_specs=anywhere,
+            scratch_shapes=[dma],
+            input_output_aliases={1: 0},
+            compiler_params=pltpu.CompilerParams(vmem_limit_bytes=8 * 2 ** 20),
+            cost_estimate=pl.CostEstimate(flops=10 ** 7, bytes_accessed=4 * late.size, transcendentals=0),
+        )(late, glo_v_out)
+        return hidden_out, loc_k_out, loc_v_out, glo_k_out, glo_v_out
 
     return jax.shard_map(device_step, mesh=mesh, in_specs=in_specs, out_specs=out_specs, check_vma=False)

time: 1160 us -> 1100 us (0.948)
  Pallas kernels: 1150 us -> 1080 us
  waiting for transfers between devices: 0 us -> 13.3 us
    pallas_call x1, Pallas kernels: 1090 us -> 1030 us  [device_step(): pl.pallas_call(move_kernel, out_shape=(loc_land, loc_land, glo_land, glo_...]
    ppermute x0 -> x1, waiting for transfers between devices: none -> 13.3 us  [device_step(): late = lax.ppermute(later, 'a', [(2, 0), (3, 1)])]
  transfers between devices with their start and end apart: 0 -> 1, of which waited for: 0 -> 1; matrix products, arithmetic and copies ran while one was open for 0% -> 0% of each run, Pallas kernels for 0% -> 5%
where the time goes in v2:
time: 1100 us
  Pallas kernels  1080 us (98%)
  waiting for transfers between devices  13.3 us (1%)
    pallas_call x1, Pallas kernels, device_step(): pl.pallas_call(move_kernel, out_shape=(loc_land, loc_land, glo_land, glo_...  1030 us
    pallas_call x1, Pallas kernels, device_step(): pl.pallas_call(write_kernel, out_shape=(jax.ShapeDtypeStruct((ROWS, model...  57.5 us
  transfers between devices with their start and end apart: 1, of which 1 were waited for; matrix products, arithmetic and copies ran while one was open for 0% of the time, Pallas kernels for 5%

profile of v2, /device:TPU:0, one launch (start us, length us, event | category | flops | bytes accessed | tf_op | source)
XLA Modules:
  0.0 1099.5 jit_solution(7862446323159002880)
XLA Ops:
  0.6 1025.1 %shard_map.209 = (bf16[8,1,4096,256]{3,2,1,0:T(8,128)(2,1)}, bf16[8,1,4096,256]{3,2,1,0:T(8,128)(2,1)}, bf16[8,1,6144,256]{3,2,1,0:T(8,128)(2,1)}, bf16[8,1,6144...) custom-call(bf16[8,2560]{1,0:T(8,128)(2,1)} %hid.1, ...), custom_call_target="tpu_custom_call" | custom-call | tf_op jit(solution)/shard_map/pallas_call | solution.py:373
  1025.7 1.3 collective-permute-start
  1027.0 57.5 %shard_map.210 = (bf16[8,2560]{1,0:T(8,128)(2,1)}, bf16[8,1,4096,256]{3,2,1,0:T(8,128)(2,1)}, bf16[8,1,4096,256]{3,2,1,0:T(8,128)(2,1)}, bf16[8,1,6656,256]{3,2,1,0:T(8,128)(2,1)}, bf16[8,1,6656,256]{3,2,1,0:T(8,128)(2,1)}) custom-call(bf16[8,2560]{1,0:T(8,128)(2,1)} %get-tuple-element.17.hid, bf16[4,8,256]{2,1,0:T(8,128)(2,1)} %get-tuple-element.18.new_kv, ...), custom_call_target="tpu_custom_call" | custom-call | flops 1000000000 | bytes 180000000 | tf_op jit(solution)/shard_map/pallas_call | solution.py:395
  1084.5 13.3 %collective-permute-done.late = bf16[4,1536,256]{2,1,0:T(8,128)(2,1)S(1)} collective-permute-done((bf16[4,1536,256]{2,1,0:T(8,128)(2,1)}, bf16[4,1536,256]{2,1,0:T(8,128)(2,1)S(1)}, u32[]{:S(2)}, u32[]{:S(2)}) %collective-permute-start) | collective-permute-done | bytes 3145760 | tf_op jit(solution)/shard_map/ppermute | solution.py:394
  1097.9 1.7 shard_map.211
Async XLA Ops:
  1025.7 72.1 %collective-permute-start = (bf16[4,1536,256]{2,1,0:T(8,128)(2,1)}, bf16[4,1536,256]{2,1,0:T(8,128)(2,1)S(1)}, u32[]{:S(2)}, u32[]{:S(2)}) collective-permute-start(bf16[4,1536,256]{2,1,0:T(8,128)(2,1)} %get-tuple-element.27), channel_id=1, source_target_pairs={{2,0},{3,1},{6,4},{7,5}} | collective-permute-start | bytes 9437192 | tf_op jit(solution)/shard_map/ppermute | solution.py:394

commit v3 on v1

--- a/solution.py
+++ b/solution.py
@@ -24,7 +24,7 @@
 FIRST_UNIT = (SEQ - WINDOW) // UNIT
 STEPS = 4 * ROWS * PER
 DEPTH = 2
-LEFT = 0
+LATE = (5, 4)
 MESH = pl.DeviceIdType.MESH
 LOW = -1e30
 
@@ -35,17 +35,17 @@
 
 def norm(hidden, gain):
     mean_sq = jnp.mean(hidden * hidden, axis=-1, keepdims=True)
-    return hidden * lax.rsqrt(mean_sq + NORM_EPS) * (1.0 + gain.astype(jnp.float32))
+    return hidden * lax.rsqrt(mean_sq + NORM_EPS) * (1.0 + gain.astype(jnp.float32).reshape(1, -1))
 
 
 def softcap(scores):
     return SOFTCAP * jnp.tanh(scores * (HEAD ** -0.5) / SOFTCAP)
 
 
-def move_kernel(hid, trig, lpre, lpost, gpre, gpost, lk, lv, gk, gv, lwq, lwk, lwv, lwo, gwq, gwk, gwv, gwo,
-                land_lk, land_lv, land_gk, land_gv, hid_out, new_kv,
-                wq, wk, wv, wo, kvbuf, qbuf, part, precv, ybuf,
-                bulk_send, loc_recv, glo_recv, w_sem, kv_sem, ex_send, ex_recv):
+def move_kernel(hid_in, trig_in, lpre_in, lpost_in, gpre_in, gpost_in, lk, lv, gk, gv, lwq, lwk, lwv, lwo, gwq, gwk, gwv, gwo,
+                land_lk, land_lv, land_gk, land_gv, hid_out, new_out, late_a, late_b,
+                hid, trig, lpre, lpost, gpre, gpost, new_kv, hid_end, wq, wk, wv, wo, kvbuf, qbuf, part, precv, ybuf,
+                bulk_send, loc_recv, glo_recv, w_sem, kv_sem, ex_send, ex_recv, late_sem, tail_send, small_sem, out_sem):
     dp = lax.axis_index("dp")
     me = lax.axis_index("a")
     dest = peers(me)
@@ -57,17 +57,21 @@
         pl.semaphore_signal(barrier, inc=1, device_id=(dp, peer), device_id_type=MESH)
     pl.semaphore_wait(barrier, 3)
 
+    def coords(step):
+        c = (step // (ROWS * PER) + 2 - 2 * (me // 2)) % 4
+        return c, (step // PER) % ROWS, step % PER
+
     def valid(step, k):
-        c, r, j = step // (ROWS * PER), (step // PER) % ROWS, step % PER
+        c, r, j = coords(step)
         in_window = jnp.logical_or(c >= 2, PER * me + j >= FIRST_UNIT)
         ok = jnp.logical_and(step >= 0, in_window)
-        if k == 1 and LEFT:
-            later = jnp.logical_and(jnp.logical_and(c == 3, r >= ROWS - LEFT), me >= 2)
-            ok = jnp.logical_and(ok, jnp.logical_not(later))
+        if k == 1:
+            late = jnp.logical_and(jnp.logical_and(c == 3, r >= ROWS - LATE[0]), me >= 2)
+            ok = jnp.logical_and(ok, jnp.logical_not(late))
         return ok
 
     def pump(step):
-        c, r, j = step // (ROWS * PER), (step // PER) % ROWS, step % PER
+        c, r, j = coords(step)
         slot = step % DEPTH
         for k in range(3):
             @pl.when(valid(step - DEPTH, k))
@@ -107,10 +111,16 @@
         (lwq, wq.at[0]), (lwk, wk.at[0]), (lwv, wv.at[0]), (lwo, wo.at[0]),
         (gwq, wq.at[1]), (gwk, wk.at[1]), (gwv, wv.at[1]), (gwo, wo.at[1])))]
 
+    small = [pltpu.make_async_copy(src, dst, small_sem.at[i]) for i, (src, dst) in enumerate((
+        (hid_in, hid), (trig_in, trig), (lpre_in, lpre), (lpost_in, lpost),
+        (gpre_in, gpre), (gpost_in, gpost)))]
+
     pump(0)
-    for copy in weights:
+    pump(1)
+    for copy in small + weights:
         copy.start()
-    pump(1)
+    for copy in small:
+        copy.wait()
 
     cosine, sine = trig[0:1, :], trig[1:2, :]
 
@@ -214,13 +224,54 @@
     part[...] = jnp.zeros_like(part)
     hidden, step = layer(0, hid[...].astype(jnp.float32), lk, lv, lpre, lpost, 2)
     hidden, step = layer(1, hidden.astype(jnp.float32), gk, gv, gpre, gpost, step)
-    hid_out[...] = hidden
+    hid_end[...] = hidden
+    outs = (pltpu.make_async_copy(hid_end, hid_out, out_sem.at[0]), pltpu.make_async_copy(new_kv, new_out, out_sem.at[1]))
+    for copy in outs:
+        copy.start()
+    for copy in outs:
+        copy.wait()
+
+    for late, target, rows in ((late_a, 0, LATE[0]), (late_b, 1, LATE[1])):
+        @pl.when(me == target + 2)
+        def _():
+            def late_in(r):
+                return pltpu.make_async_copy(gv.at[ROWS - rows + r, target], kvbuf.at[(r // 2) % 2, r % 2], late_sem.at[0, r])
+
+            def late_out(r):
+                return pltpu.make_async_copy(kvbuf.at[(r // 2) % 2, r % 2], late.at[r], late_sem.at[1, r])
+
+            for r in range(rows):
+                if r >= 4:
+                    late_out(r - 4).wait()
+                late_in(r).start()
+                if r >= 1:
+                    late_in(r - 1).wait()
+                    late_out(r - 1).start()
+            late_in(rows - 1).wait()
+            late_out(rows - 1).start()
+            for r in range(max(rows - 4, 0), rows):
+                late_out(r).wait()
 
     def rest(s, carry):
         pump(s)
         return carry
 
     lax.fori_loop(step, STEPS, rest, 0)
+
+    def tail(r, j):
+        unit = PER * me + j
+        return pltpu.make_async_remote_copy(
+            src_ref=gv.at[r, dest[1], pl.ds(j * UNIT, UNIT)],
+            dst_ref=land_gv.at[r, 0, pl.ds(pl.multiple_of(unit * UNIT, UNIT), UNIT)],
+            send_sem=tail_send.at[r - ROWS + LATE[0], j], recv_sem=glo_recv.at[1, unit],
+            device_id=(dp, dest[1]), device_id_type=MESH)
+
+    tails = [(r, j) for r in range(ROWS - LATE[0], ROWS - LATE[1]) for j in range(PER)]
+
+    @pl.when(me == 3)
+    def _():
+        for piece in tails:
+            tail(*piece).start()
 
     for s in range(STEPS - DEPTH, STEPS):
         for k in range(3):
@@ -230,6 +281,12 @@
                     src_ref=gk.at[0, 0, pl.ds(0, UNIT)], dst_ref=land_gk.at[0, 0, pl.ds(0, UNIT)],
                     send_sem=bulk_send.at[k, s % DEPTH], recv_sem=glo_recv.at[0, 0],
                     device_id=(dp, dest[k]), device_id_type=MESH).wait_send()
+
+    @pl.when(me == 3)
+    def _():
+        for piece in tails:
+            tail(*piece).wait_send()
+
     for i in range(4):
         for u in range(LOC_UNITS if i < 2 else GLO_UNITS):
             owner = (u if i >= 2 or u >= FIRST_UNIT else u + LOC_UNITS) // PER
@@ -241,12 +298,12 @@
                     src_ref=view, dst_ref=view, send_sem=bulk_send.at[0, 0], recv_sem=sem,
                     device_id=(dp, dest[0]), device_id_type=MESH).wait_recv()
 
-            if LEFT and i == 3 and owner >= 2:
+            if i == 3 and owner >= 2:
                 short = me == owner - 2
 
                 @pl.when(short)
                 def _():
-                    await_rows(ROWS - LEFT)
+                    await_rows(ROWS - LATE[owner - 2])
 
                 @pl.when(jnp.logical_and(me != owner, jnp.logical_not(short)))
                 def _():
@@ -317,6 +374,18 @@
         store(n).wait()
 
 
+def late_kernel(late_a, late_b, old, out, sem):
+    me = lax.axis_index("a")
+    for target, late in enumerate((late_a, late_b)):
+        rows = LATE[target]
+
+        @pl.when(me == target)
+        def _():
+            copy = pltpu.make_async_copy(late, out.at[pl.ds(ROWS - rows, rows), 0, pl.ds((target + 2) * BLOCK, BLOCK)], sem)
+            copy.start()
+            copy.wait()
+
+
 def trig_table():
     half = HEAD // 2
     inv_freq = ROPE_BASE ** (-2.0 * np.arange(half) / HEAD)
@@ -337,17 +406,21 @@
 
     def device_step(hidden_in, loc_k, loc_v, glo_k, glo_v, loc_wq, loc_wk, loc_wv, loc_wo, loc_pre, loc_post, glo_wq, glo_wk, glo_wv, glo_wo, glo_pre, glo_post):
         model = hidden_in.shape[1]
-        gains = [g.reshape(1, model) for g in (loc_pre, loc_post, glo_pre, glo_post)]
+        gains = [loc_pre, loc_post, glo_pre, glo_post]
         loc_land = jax.ShapeDtypeStruct((ROWS, 1, WINDOW, HEAD), bf16)
         glo_land = jax.ShapeDtypeStruct((ROWS, 1, SEQ, HEAD), bf16)
         dma = pltpu.SemaphoreType.DMA
         moved = pl.pallas_call(
             move_kernel,
             out_shape=(loc_land, loc_land, glo_land, glo_land,
-                       jax.ShapeDtypeStruct((ROWS, model), bf16), jax.ShapeDtypeStruct((4, ROWS, HEAD), bf16)),
-            in_specs=[vmem] * 6 + [anywhere] * 12,
-            out_specs=(anywhere,) * 4 + (vmem, vmem),
+                       jax.ShapeDtypeStruct((ROWS, model), bf16), jax.ShapeDtypeStruct((4, ROWS, HEAD), bf16),
+                       jax.ShapeDtypeStruct((LATE[0], BLOCK, HEAD), bf16), jax.ShapeDtypeStruct((LATE[1], BLOCK, HEAD), bf16)),
+            in_specs=[anywhere] * 18,
+            out_specs=(anywhere,) * 8,
             scratch_shapes=[
+                pltpu.VMEM((ROWS, model), bf16), pltpu.VMEM((2, HEAD // 2), f32),
+                pltpu.VMEM((model,), bf16), pltpu.VMEM((model,), bf16), pltpu.VMEM((model,), bf16), pltpu.VMEM((model,), bf16),
+                pltpu.VMEM((4, ROWS, HEAD), bf16), pltpu.VMEM((ROWS, model), bf16),
                 pltpu.VMEM((2,) + loc_wq.shape, bf16), pltpu.VMEM((2,) + loc_wk.shape, bf16),
                 pltpu.VMEM((2,) + loc_wv.shape, bf16), pltpu.VMEM((2,) + loc_wo.shape, bf16),
                 pltpu.VMEM((2, 2, BLOCK, HEAD), bf16),
@@ -356,12 +429,15 @@
                 pltpu.VMEM((2, GROUP, 2 * ROWS, 2 * HEAD), f32),
                 pltpu.VMEM((2, GROUP, ROWS, model), bf16),
                 dma((3, DEPTH)), dma((2, LOC_UNITS)), dma((2, GLO_UNITS)), dma((8,)), dma((2, 2)),
-                dma((6, 3)), dma((6, 3))],
+                dma((6, 3)), dma((6, 3)), dma((2, LATE[0])),
+                dma((LATE[0] - LATE[1], PER)), dma((6,)), dma((2,))],
             compiler_params=pltpu.CompilerParams(collective_id=0, has_side_effects=True),
         )(hidden_in, jnp.asarray(trig_table()), *gains, loc_k, loc_v, glo_k, glo_v,
           loc_wq, loc_wk, loc_wv, loc_wo, glo_wq, glo_wk, glo_wv, glo_wo)
         land, hid, new_kv = moved[:4], moved[4], moved[5]
-        return pl.pallas_call(
+        late_a = lax.ppermute(moved[6], 'a', [(2, 0)])
+        late_b = lax.ppermute(moved[7], 'a', [(3, 1)])
+        hidden_out, loc_k_out, loc_v_out, glo_k_out, glo_v_out = pl.pallas_call(
             write_kernel,
             out_shape=(jax.ShapeDtypeStruct((ROWS, model), bf16),)
             + (jax.ShapeDtypeStruct((ROWS, 1, WINDOW, HEAD), bf16),) * 2
@@ -369,7 +445,19 @@
             in_specs=[vmem, vmem] + [anywhere] * 8,
             out_specs=(vmem,) + (anywhere,) * 4,
             scratch_shapes=[pltpu.VMEM((SLOTS, ROWS, UNIT, HEAD), bf16), dma((SLOTS,)), dma((SLOTS,))],
+            compiler_params=pltpu.CompilerParams(vmem_limit_bytes=50 * 2 ** 20),
             cost_estimate=pl.CostEstimate(flops=10 ** 9, bytes_accessed=180 * 10 ** 6, transcendentals=0),
         )(hid, new_kv, loc_k, loc_v, glo_k, glo_v, *land)
+        glo_v_out = pl.pallas_call(
+            late_kernel,
+            out_shape=jax.ShapeDtypeStruct(glo_v_out.shape, bf16),
+            in_specs=[vmem, vmem, anywhere],
+            out_specs=anywhere,
+            scratch_shapes=[dma],
+            input_output_aliases={2: 0},
+            compiler_params=pltpu.CompilerParams(vmem_limit_bytes=16 * 2 ** 20),
+            cost_estimate=pl.CostEstimate(flops=10 ** 7, bytes_accessed=4 * late_a.size, transcendentals=0),
+        )(late_a, late_b, glo_v_out)
+        return hidden_out, loc_k_out, loc_v_out, glo_k_out, glo_v_out
 
     return jax.shard_map(device_step, mesh=mesh, in_specs=in_specs, out_specs=out_specs, check_vma=False)

time: 1160 us -> 1090 us (0.940)
  Pallas kernels: 1150 us -> 1070 us
  waiting for transfers between devices: 0 us -> 22.8 us
    pallas_call x1, Pallas kernels: 1090 us -> 1010 us  [device_step(): pl.pallas_call(move_kernel, out_shape=(loc_land, loc_land, glo_land, glo_...]
    ppermute x0 -> x2, waiting for transfers between devices: none -> 22.8 us  [the longest x1 22.8 us: device_step(): late_a = lax.ppermute(moved[6], 'a', [(2, 0)])]
  transfers between devices with their start and end apart: 0 -> 2, of which waited for: 0 -> 1; matrix products, arithmetic and copies ran while one was open for 0% -> 0% of each run, Pallas kernels for 0% -> 5%
where the time goes in v3:
time: 1090 us
  Pallas kernels  1070 us (98%)
  waiting for transfers between devices  22.8 us (2%)
    pallas_call x1, Pallas kernels, device_step(): pl.pallas_call(move_kernel, out_shape=(loc_land, loc_land, glo_land, glo_...  1010 us
    pallas_call x1, Pallas kernels, device_step(): pl.pallas_call(write_kernel, out_shape=(jax.ShapeDtypeStruct((ROWS, model...  56.7 us
    ppermute x1, waiting for transfers between devices, device_step(): late_a = lax.ppermute(moved[6], 'a', [(2, 0)])  22.8 us
  transfers between devices with their start and end apart: 2, of which 1 were waited for; matrix products, arithmetic and copies ran while one was open for 0% of the time, Pallas kernels for 5%

profile of v3, /device:TPU:0, one launch (start us, length us, event | category | flops | bytes accessed | tf_op | source)
XLA Modules:
  0.0 1092.6 jit_solution(4180394396934324997)
XLA Ops:
  0.6 1006.9 %shard_map.209 = (bf16[8,1,4096,256]{3,2,1,0:T(8,128)(2,1)}, bf16[8,1,4096,256]{3,2,1,0:T(8,128)(2,1)}, bf16[8,1,6144,256]{3,2,1,0:T(8,128)(2,1)}, bf16[8,1,6144...) custom-call(bf16[8,2560]{1,0:T(8,128)(2,1)} %hid_in.1, ...), custom_call_target="tpu_custom_call" | custom-call | tf_op jit(solution)/shard_map/pallas_call | solution.py:413
  1007.5 1.3 collective-permute-start
  1008.8 0.9 collective-permute-start.1
  1009.7 0.0 copy-start
  1009.7 0.8 copy-done
  1010.5 0.0 copy-start.1
  1010.5 0.7 copy-done.1
  1011.2 56.7 %shard_map.210 = (bf16[8,2560]{1,0:T(8,128)(2,1)}, bf16[8,1,4096,256]{3,2,1,0:T(8,128)(2,1)}, bf16[8,1,4096,256]{3,2,1,0:T(8,128)(2,1)}, bf16[8,1,6656,256]{3,2,1,0:T(8,128)(2,1)}, bf16[8,1,6656,256]{3,2,1,0:T(8,128)(2,1)}) custom-call(bf16[8,2560]{1,0:T(8,128)(2,1)S(1)} %copy-done, bf16[4,8,256]{2,1,0:T(8,128)(2,1)S(1)} %copy-done.1, ...), custom_call_target="tpu_custom_call" | custom-call | flops 1000000000 | bytes 180000000 | tf_op jit(solution)/shard_map/pallas_call | solution.py:440
  1067.9 0.0 collective-permute-done.1.late_b
  1067.9 22.8 %collective-permute-done.late_a = bf16[5,1536,256]{2,1,0:T(8,128)(2,1)S(1)} collective-permute-done((bf16[5,1536,256]{2,1,0:T(8,128)(2,1)}, bf16[5,1536,256]{2,1,0:T(8,128)(2,1)S(1)}, u32[]{:S(2)}, u32[]{:S(2)}) %collective-permute-start) | collective-permute-done | bytes 3932192 | tf_op jit(solution)/shard_map/ppermute | solution.py:438
  1090.7 1.9 shard_map.211
Async XLA Ops:
  1007.5 83.2 %collective-permute-start = (bf16[5,1536,256]{2,1,0:T(8,128)(2,1)}, bf16[5,1536,256]{2,1,0:T(8,128)(2,1)S(1)}, u32[]{:S(2)}, u32[]{:S(2)}) collective-permute-start(bf16[5,1536,256]{2,1,0:T(8,128)(2,1)} %get-tuple-element.28), channel_id=1, source_target_pairs={{2,0},{6,4}} | collective-permute-start | bytes 11796488 | tf_op jit(solution)/shard_map/ppermute | solution.py:438
  1008.8 59.1 %collective-permute-start.1 = (bf16[4,1536,256]{2,1,0:T(8,128)(2,1)}, bf16[4,1536,256]{2,1,0:T(8,128)(2,1)S(1)}, u32[]{:S(2)}, u32[]{:S(2)}) collective-permute-start(bf16[4,1536,256]{2,1,0:T(8,128)(2,1)} %get-tuple-element.29), channel_id=1, source_target_pairs={{3,1},{7,5}} | collective-permute-start | bytes 9437192 | tf_op jit(solution)/shard_map/ppermute | solution.py:439
  1009.7 0.8 copy-start
  1010.5 0.7 copy-start.1

commit v4 on v3

--- a/solution.py
+++ b/solution.py
@@ -26,6 +26,7 @@
 DEPTH = 2
 LATE = (5, 4)
 MESH = pl.DeviceIdType.MESH
+STAT = 64
 LOW = -1e30
 
 
@@ -44,7 +45,7 @@
 
 def move_kernel(hid_in, trig_in, lpre_in, lpost_in, gpre_in, gpost_in, lk, lv, gk, gv, lwq, lwk, lwv, lwo, gwq, gwk, gwv, gwo,
                 land_lk, land_lv, land_gk, land_gv, hid_out, new_out, late_a, late_b,
-                hid, trig, lpre, lpost, gpre, gpost, new_kv, hid_end, wq, wk, wv, wo, kvbuf, qbuf, part, precv, ybuf,
+                hid, trig, lpre, lpost, gpre, gpost, new_kv, hid_end, wq, wk, wv, wo, kvbuf, qbuf, part, precv, pair, ybuf, hbuf,
                 bulk_send, loc_recv, glo_recv, w_sem, kv_sem, ex_send, ex_recv, late_sem, tail_send, small_sem, out_sem):
     dp = lax.axis_index("dp")
     me = lax.axis_index("a")
@@ -93,19 +94,10 @@
                         send_sem=bulk_send.at[k, slot], recv_sem=sem,
                         device_id=(dp, dest[k]), device_id_type=MESH).start()
 
-    def exchange(index, src_of, dst):
-        copies = []
-        for k in range(3):
-            copies.append(pltpu.make_async_remote_copy(
-                src_ref=src_of(dest[k]), dst_ref=dst.at[me], send_sem=ex_send.at[index, k], recv_sem=ex_recv.at[index, k],
-                device_id=(dp, dest[k]), device_id_type=MESH))
-        for copy in copies:
-            copy.start()
-        return copies
-
-    def finish(copies):
-        for copy in copies:
-            copy.wait()
+    def send(index, k, src, dst):
+        return pltpu.make_async_remote_copy(
+            src_ref=src, dst_ref=dst, send_sem=ex_send.at[index], recv_sem=ex_recv.at[index],
+            device_id=(dp, dest[k]), device_id_type=MESH)
 
     weights = [pltpu.make_async_copy(src, dst, w_sem.at[i]) for i, (src, dst) in enumerate((
         (lwq, wq.at[0]), (lwk, wk.at[0]), (lwv, wv.at[0]), (lwo, wo.at[0]),
@@ -144,9 +136,17 @@
         new_kv[2 * index + 1] = new_v
         own_q = qbuf.at[index]
         own_q[me] = q
-        sent = exchange(3 * index, lambda peer: own_q.at[me], own_q)
+        base = 9 * index
+        near = send(base, 0, own_q.at[me], own_q.at[me])
+        far = send(base + 1, 1, own_q.at[me], own_q.at[me])
+        near.start()
+        far.start()
         pump(step)
-        finish(sent)
+        far.wait()
+        onward = send(base + 2, 0, own_q.at[dest[1]], own_q.at[dest[1]])
+        onward.start()
+        near.wait()
+        onward.wait()
 
         def fetch(item, slot):
             h, r = item // ROWS, item % ROWS
@@ -182,8 +182,8 @@
             total = jnp.sum(e, axis=-1, keepdims=True)
             copy_v.wait()
             out = jnp.dot(e.astype(jnp.bfloat16), kvbuf[slot, 1], preferred_element_type=jnp.float32)
-            wide = jnp.concatenate([out, jnp.broadcast_to(top, (2 * ROWS, 128)),
-                                    jnp.broadcast_to(total, (2 * ROWS, 128))], axis=-1)
+            wide = jnp.concatenate([out, jnp.broadcast_to(top, (2 * ROWS, STAT)),
+                                    jnp.broadcast_to(total, (2 * ROWS, STAT))], axis=-1)
             row = lax.broadcasted_iota(jnp.int32, wide.shape, 0) % ROWS
             part[index, h] = jnp.where(row == r, wide, part[index, h])
             return carry
@@ -191,35 +191,94 @@
         lax.fori_loop(0, items, body, 0)
         step = step + 1 + items
 
-        sent = exchange(3 * index + 1, lambda peer: part.at[index, peer], precv.at[index])
-        precv[index, me] = part[index, me]
-        pump(step)
+        mine = part.at[index]
+        theirs = precv.at[index]
+        near = (send(base + 3, 0, mine.at[dest[0]], theirs.at[0]), send(base + 4, 0, mine.at[dest[2]], theirs.at[1]))
+        for copy in near:
+            copy.start()
         new_k2 = jnp.concatenate([new_k, new_k], axis=0).astype(jnp.float32)
         new_v2 = jnp.concatenate([new_v, new_v], axis=0).astype(jnp.float32)
         new_s = softcap(jnp.sum(q.astype(jnp.float32) * new_k2, axis=-1, keepdims=True))
-        finish(sent)
+        for copy in near:
+            copy.wait()
+
+        def split(block):
+            return block[:, :HEAD], block[:, HEAD:HEAD + 1], block[:, HEAD + STAT:HEAD + STAT + 1]
+
+        o_a, m_a, l_a = split(mine[dest[1]])
+        o_b, m_b, l_b = split(theirs[1])
+        top = jnp.maximum(m_a, m_b)
+        scale_a, scale_b = jnp.exp(m_a - top), jnp.exp(m_b - top)
+        pair[index] = jnp.concatenate(
+            [o_a * scale_a + o_b * scale_b, jnp.broadcast_to(top, (2 * ROWS, STAT)),
+             jnp.broadcast_to(l_a * scale_a + l_b * scale_b, (2 * ROWS, STAT))], axis=-1)
+        far = send(base + 5, 1, pair.at[index], theirs.at[2])
+        far.start()
+        pump(step)
+        far.wait()
+        blocks = [split(mine[me]), split(theirs[0]), split(theirs[2])]
         top = new_s
-        for d in range(GROUP):
-            top = jnp.maximum(top, precv[index, d, :, HEAD:HEAD + 1])
+        for _, m, _ in blocks:
+            top = jnp.maximum(top, m)
         new_e = jnp.exp(new_s - top)
         total = new_e
         acc = new_e.astype(jnp.bfloat16).astype(jnp.float32) * new_v2
-        for d in range(GROUP):
-            scale = jnp.exp(precv[index, d, :, HEAD:HEAD + 1] - top)
-            total = total + scale * precv[index, d, :, HEAD + 128:HEAD + 129]
-            acc = acc + scale * precv[index, d, :, :HEAD]
+        for o, m, l in blocks:
+            scale = jnp.exp(m - top)
+            total = total + scale * l
+            acc = acc + scale * o
         att = (acc / total).astype(jnp.bfloat16)
         own = jnp.concatenate([att[:ROWS], att[ROWS:]], axis=-1)
         y = jnp.dot(own, wo[index], preferred_element_type=jnp.float32).astype(jnp.bfloat16)
         y_ref = ybuf.at[index]
         y_ref[me] = y
-        sent = exchange(3 * index + 2, lambda peer: y_ref.at[me], y_ref)
+        near = send(base + 6, 0, y_ref.at[me], y_ref.at[me])
+        far = [send(base + 6 + k, k, y_ref.at[me], y_ref.at[me]) for k in (1, 2)]
+        half = hbuf.at[index]
+        side = me % 2
+        back = send(18 + 2 * index, 1, half.at[side], half.at[side])
+        swap = send(19 + 2 * index, 0, half.at[side], half.at[side])
+
+        @pl.when(me >= 2)
+        def _():
+            near.start()
+
+        @pl.when(me < 2)
+        def _():
+            for copy in far:
+                copy.start()
+
         pump(step + 1)
-        finish(sent)
-        summed = y_ref[0].astype(jnp.float32)
-        for d in range(1, GROUP):
-            summed = summed + y_ref[d].astype(jnp.float32)
-        return (hidden + norm(summed, post[...])).astype(jnp.bfloat16), step + 2
+
+        @pl.when(me >= 2)
+        def _():
+            near.wait_recv()
+            for copy in far:
+                copy.wait_recv()
+            summed = y_ref[0].astype(jnp.float32)
+            for d in range(1, GROUP):
+                summed = summed + y_ref[d].astype(jnp.float32)
+            after = (hidden + norm(summed, post[...])).astype(jnp.bfloat16)
+            half[0] = after[:, :after.shape[1] // 2]
+            half[1] = after[:, after.shape[1] // 2:]
+            back.start()
+
+        pump(step + 2)
+
+        @pl.when(me >= 2)
+        def _():
+            near.wait_send()
+            back.wait_send()
+
+        @pl.when(me < 2)
+        def _():
+            for copy in far:
+                copy.wait_send()
+            back.wait_recv()
+            swap.start()
+            swap.wait()
+
+        return jnp.concatenate([half[0], half[1]], axis=-1), step + 3
 
     part[...] = jnp.zeros_like(part)
     hidden, step = layer(0, hid[...].astype(jnp.float32), lk, lv, lpre, lpost, 2)
@@ -425,11 +484,12 @@
                 pltpu.VMEM((2,) + loc_wv.shape, bf16), pltpu.VMEM((2,) + loc_wo.shape, bf16),
                 pltpu.VMEM((2, 2, BLOCK, HEAD), bf16),
                 pltpu.VMEM((2, GROUP, 2 * ROWS, HEAD), bf16),
-                pltpu.VMEM((2, GROUP, 2 * ROWS, 2 * HEAD), f32),
-                pltpu.VMEM((2, GROUP, 2 * ROWS, 2 * HEAD), f32),
-                pltpu.VMEM((2, GROUP, ROWS, model), bf16),
+                pltpu.VMEM((2, GROUP, 2 * ROWS, HEAD + 2 * STAT), f32),
+                pltpu.VMEM((2, 3, 2 * ROWS, HEAD + 2 * STAT), f32),
+                pltpu.VMEM((2, 2 * ROWS, HEAD + 2 * STAT), f32),
+                pltpu.VMEM((2, GROUP, ROWS, model), bf16), pltpu.VMEM((2, 2, ROWS, model // 2), bf16),
                 dma((3, DEPTH)), dma((2, LOC_UNITS)), dma((2, GLO_UNITS)), dma((8,)), dma((2, 2)),
-                dma((6, 3)), dma((6, 3)), dma((2, LATE[0])),
+                dma((22,)), dma((22,)), dma((2, LATE[0])),
                 dma((LATE[0] - LATE[1], PER)), dma((6,)), dma((2,))],
             compiler_params=pltpu.CompilerParams(collective_id=0, has_side_effects=True),
         )(hidden_in, jnp.asarray(trig_table()), *gains, loc_k, loc_v, glo_k, glo_v,

time: 1090 us -> 1090 us (level)
  no operation moved by 1% of the time
where the time goes in v4:
time: 1090 us
  Pallas kernels  1060 us (97%)
  waiting for transfers between devices  22.7 us (2%)
    pallas_call x1, Pallas kernels, device_step(): pl.pallas_call(move_kernel, out_shape=(loc_land, loc_land, glo_land, glo_...  1000 us
    pallas_call x1, Pallas kernels, device_step(): pl.pallas_call(write_kernel, out_shape=(jax.ShapeDtypeStruct((ROWS, model...  56.7 us
    ppermute x1, waiting for transfers between devices, device_step(): late_a = lax.ppermute(moved[6], 'a', [(2, 0)])  22.7 us
  transfers between devices with their start and end apart: 2, of which 1 were waited for; matrix products, arithmetic and copies ran while one was open for 0% of the time, Pallas kernels for 5%

profile of v4, /device:TPU:0, one launch (start us, length us, event | category | flops | bytes accessed | tf_op | source)
XLA Modules:
  0.0 1087.9 jit_solution(5346178578633275192)
XLA Ops:
  0.6 1002.2 %shard_map.209 = (bf16[8,1,4096,256]{3,2,1,0:T(8,128)(2,1)}, bf16[8,1,4096,256]{3,2,1,0:T(8,128)(2,1)}, bf16[8,1,6144,256]{3,2,1,0:T(8,128)(2,1)}, bf16[8,1,6144...) custom-call(bf16[8,2560]{1,0:T(8,128)(2,1)} %hid_in.1, ...), custom_call_target="tpu_custom_call" | custom-call | tf_op jit(solution)/shard_map/pallas_call | solution.py:472
  1002.9 1.3 collective-permute-start
  1004.2 0.9 collective-permute-start.1
  1005.0 0.0 copy-start
  1005.1 0.8 copy-done
  1005.8 0.0 copy-start.1
  1005.8 0.7 copy-done.1
  1006.5 56.7 %shard_map.210 = (bf16[8,2560]{1,0:T(8,128)(2,1)}, bf16[8,1,4096,256]{3,2,1,0:T(8,128)(2,1)}, bf16[8,1,4096,256]{3,2,1,0:T(8,128)(2,1)}, bf16[8,1,6656,256]{3,2,1,0:T(8,128)(2,1)}, bf16[8,1,6656,256]{3,2,1,0:T(8,128)(2,1)}) custom-call(bf16[8,2560]{1,0:T(8,128)(2,1)S(1)} %copy-done, bf16[4,8,256]{2,1,0:T(8,128)(2,1)S(1)} %copy-done.1, ...), custom_call_target="tpu_custom_call" | custom-call | flops 1000000000 | bytes 180000000 | tf_op jit(solution)/shard_map/pallas_call | solution.py:500
  1063.2 0.0 collective-permute-done.1.late_b
  1063.3 22.7 %collective-permute-done.late_a = bf16[5,1536,256]{2,1,0:T(8,128)(2,1)S(1)} collective-permute-done((bf16[5,1536,256]{2,1,0:T(8,128)(2,1)}, bf16[5,1536,256]{2,1,0:T(8,128)(2,1)S(1)}, u32[]{:S(2)}, u32[]{:S(2)}) %collective-permute-start) | collective-permute-done | bytes 3932192 | tf_op jit(solution)/shard_map/ppermute | solution.py:498
  1086.0 1.9 shard_map.211
Async XLA Ops:
  1002.9 83.1 %collective-permute-start = (bf16[5,1536,256]{2,1,0:T(8,128)(2,1)}, bf16[5,1536,256]{2,1,0:T(8,128)(2,1)S(1)}, u32[]{:S(2)}, u32[]{:S(2)}) collective-permute-start(bf16[5,1536,256]{2,1,0:T(8,128)(2,1)} %get-tuple-element.28), channel_id=1, source_target_pairs={{2,0},{6,4}} | collective-permute-start | bytes 11796488 | tf_op jit(solution)/shard_map/ppermute | solution.py:498
  1004.2 59.1 %collective-permute-start.1 = (bf16[4,1536,256]{2,1,0:T(8,128)(2,1)}, bf16[4,1536,256]{2,1,0:T(8,128)(2,1)S(1)}, u32[]{:S(2)}, u32[]{:S(2)}) collective-permute-start(bf16[4,1536,256]{2,1,0:T(8,128)(2,1)} %get-tuple-element.29), channel_id=1, source_target_pairs={{3,1},{7,5}} | collective-permute-start | bytes 9437192 | tf_op jit(solution)/shard_map/ppermute | solution.py:499
  1005.0 0.8 copy-start
  1005.8 0.7 copy-start.1

commit v5 on v4

--- a/solution.py
+++ b/solution.py
@@ -44,14 +44,22 @@
 
 
 def move_kernel(hid_in, trig_in, lpre_in, lpost_in, gpre_in, gpost_in, lk, lv, gk, gv, lwq, lwk, lwv, lwo, gwq, gwk, gwv, gwo,
-                land_lk, land_lv, land_gk, land_gv, hid_out, new_out, late_a, late_b,
-                hid, trig, lpre, lpost, gpre, gpost, new_kv, hid_end, wq, wk, wv, wo, kvbuf, qbuf, part, precv, pair, ybuf, hbuf,
-                bulk_send, loc_recv, glo_recv, w_sem, kv_sem, ex_send, ex_recv, late_sem, tail_send, small_sem, out_sem):
+                land_lk, land_lv, land_gk, land_gv, hid_out, new_out, late_a, late_b, late_c,
+                hid, trig, lpre, lpost, gpre, gpost, new_kv, hid_end, wq, wk, wv, wo, kvbuf, qbuf, part, precv, pair, att, ybuf, hbuf,
+                bulk_send, loc_recv, glo_recv, w_sem, kv_sem, ex_send, ex_recv, late_sem, tail_send, small_sem, out_sem, first_sem):
     dp = lax.axis_index("dp")
     me = lax.axis_index("a")
     dest = peers(me)
     caches = (lk, lv, gk, gv)
     lands = (land_lk, land_lv, land_gk, land_gv)
+
+    first = [pltpu.make_async_copy(lk.at[0, dest[k], pl.ds(0, UNIT)], kvbuf.at[0, k - 1, pl.ds(0, UNIT)], first_sem.at[k - 1])
+             for k in (1, 2)]
+
+    @pl.when(me >= 2)
+    def _():
+        for copy in first:
+            copy.start()
 
     barrier = pltpu.get_barrier_semaphore()
     for peer in dest:
@@ -71,7 +79,7 @@
             ok = jnp.logical_and(ok, jnp.logical_not(late))
         return ok
 
-    def pump(step):
+    def pump(step, opening=False):
         c, r, j = coords(step)
         slot = step % DEPTH
         for k in range(3):
@@ -86,7 +94,11 @@
             place = unit % LOC_UNITS if i < 2 else unit
             sem = loc_recv.at[i, place] if i < 2 else glo_recv.at[i - 2, place]
             for k in range(3):
-                @pl.when(jnp.logical_and(c == i, valid(step, k)))
+                now = jnp.logical_and(c == i, valid(step, k))
+                if opening and k:
+                    now = jnp.logical_and(now, me < 2)
+
+                @pl.when(now)
                 def _():
                     pltpu.make_async_remote_copy(
                         src_ref=caches[i].at[r, dest[k], pl.ds(pl.multiple_of(j * UNIT, UNIT), UNIT)],
@@ -107,7 +119,18 @@
         (hid_in, hid), (trig_in, trig), (lpre_in, lpre), (lpost_in, lpost),
         (gpre_in, gpre), (gpost_in, gpost)))]
 
-    pump(0)
+    @pl.when(me >= 2)
+    def _():
+        place = (PER * me) % LOC_UNITS
+        for k in (1, 2):
+            first[k - 1].wait()
+            pltpu.make_async_remote_copy(
+                src_ref=kvbuf.at[0, k - 1, pl.ds(0, UNIT)],
+                dst_ref=land_lk.at[0, 0, pl.ds(pl.multiple_of(place * UNIT, UNIT), UNIT)],
+                send_sem=bulk_send.at[k, 0], recv_sem=loc_recv.at[0, place],
+                device_id=(dp, dest[k]), device_id_type=MESH).start()
+
+    pump(0, opening=True)
     pump(1)
     for copy in small + weights:
         copy.start()
@@ -136,7 +159,7 @@
         new_kv[2 * index + 1] = new_v
         own_q = qbuf.at[index]
         own_q[me] = q
-        base = 9 * index
+        base = 11 * index
         near = send(base, 0, own_q.at[me], own_q.at[me])
         far = send(base + 1, 1, own_q.at[me], own_q.at[me])
         near.start()
@@ -199,45 +222,77 @@
         new_k2 = jnp.concatenate([new_k, new_k], axis=0).astype(jnp.float32)
         new_v2 = jnp.concatenate([new_v, new_v], axis=0).astype(jnp.float32)
         new_s = softcap(jnp.sum(q.astype(jnp.float32) * new_k2, axis=-1, keepdims=True))
+        new = (new_v2, new_s, jnp.ones_like(new_s))
         for copy in near:
             copy.wait()
 
         def split(block):
             return block[:, :HEAD], block[:, HEAD:HEAD + 1], block[:, HEAD + STAT:HEAD + STAT + 1]
 
-        o_a, m_a, l_a = split(mine[dest[1]])
-        o_b, m_b, l_b = split(theirs[1])
-        top = jnp.maximum(m_a, m_b)
-        scale_a, scale_b = jnp.exp(m_a - top), jnp.exp(m_b - top)
-        pair[index] = jnp.concatenate(
-            [o_a * scale_a + o_b * scale_b, jnp.broadcast_to(top, (2 * ROWS, STAT)),
-             jnp.broadcast_to(l_a * scale_a + l_b * scale_b, (2 * ROWS, STAT))], axis=-1)
-        far = send(base + 5, 1, pair.at[index], theirs.at[2])
-        far.start()
+        def merge(blocks):
+            top = blocks[0][1]
+            for _, m, _ in blocks[1:]:
+                top = jnp.maximum(top, m)
+            acc, total = 0.0, 0.0
+            for o, m, l in blocks:
+                scale = jnp.exp(m - top)
+                acc = acc + scale * o
+                total = total + scale * l
+            return acc, top, total
+
+        def packed(acc, top, total):
+            return jnp.concatenate([acc, jnp.broadcast_to(top, (2 * ROWS, STAT)),
+                                    jnp.broadcast_to(total, (2 * ROWS, STAT))], axis=-1)
+
+        both = [split(mine[me]), split(theirs[0]), new]
+        across = pair.at[index]
+        across[0] = packed(*merge([split(mine[dest[1]]), split(theirs[1])]))
+        across[1] = packed(*merge(both))
+        result = att.at[index]
+        far = [send(base + 5 + i, 1, across.at[i], theirs.at[2 + i]) for i in (0, 1)]
+        reply = send(base + 7, 1, result.at[1], result.at[0])
+
+        @pl.when(me < 2)
+        def _():
+            for copy in far:
+                copy.start()
+
         pump(step)
-        far.wait()
-        blocks = [split(mine[me]), split(theirs[0]), split(theirs[2])]
-        top = new_s
-        for _, m, _ in blocks:
-            top = jnp.maximum(top, m)
-        new_e = jnp.exp(new_s - top)
-        total = new_e
-        acc = new_e.astype(jnp.bfloat16).astype(jnp.float32) * new_v2
-        for o, m, l in blocks:
-            scale = jnp.exp(m - top)
-            total = total + scale * l
-            acc = acc + scale * o
-        att = (acc / total).astype(jnp.bfloat16)
-        own = jnp.concatenate([att[:ROWS], att[ROWS:]], axis=-1)
+
+        @pl.when(me >= 2)
+        def _():
+            for copy in far:
+                copy.wait_recv()
+            acc, _, total = merge(both + [split(theirs[2])])
+            result[0] = (acc / total).astype(jnp.bfloat16)
+            acc, _, total = merge([split(across[0]), split(theirs[3])])
+            result[1] = (acc / total).astype(jnp.bfloat16)
+            reply.start()
+
+        pump(step + 1)
+
+        @pl.when(me >= 2)
+        def _():
+            reply.wait_send()
+
+        @pl.when(me < 2)
+        def _():
+            for copy in far:
+                copy.wait_send()
+            reply.wait_recv()
+
+        heads = result[0]
+        step = step + 1
+        own = jnp.concatenate([heads[:ROWS], heads[ROWS:]], axis=-1)
         y = jnp.dot(own, wo[index], preferred_element_type=jnp.float32).astype(jnp.bfloat16)
         y_ref = ybuf.at[index]
         y_ref[me] = y
-        near = send(base + 6, 0, y_ref.at[me], y_ref.at[me])
-        far = [send(base + 6 + k, k, y_ref.at[me], y_ref.at[me]) for k in (1, 2)]
+        near = send(base + 8, 0, y_ref.at[me], y_ref.at[me])
+        far = [send(base + 8 + k, k, y_ref.at[me], y_ref.at[me]) for k in (1, 2)]
         half = hbuf.at[index]
         side = me % 2
-        back = send(18 + 2 * index, 1, half.at[side], half.at[side])
-        swap = send(19 + 2 * index, 0, half.at[side], half.at[side])
+        back = send(22 + 2 * index, 1, half.at[side], half.at[side])
+        swap = send(23 + 2 * index, 0, half.at[side], half.at[side])
 
         @pl.when(me >= 2)
         def _():
@@ -297,7 +352,8 @@
                 return pltpu.make_async_copy(gv.at[ROWS - rows + r, target], kvbuf.at[(r // 2) % 2, r % 2], late_sem.at[0, r])
 
             def late_out(r):
-                return pltpu.make_async_copy(kvbuf.at[(r // 2) % 2, r % 2], late.at[r], late_sem.at[1, r])
+                target_ref = late.at[r] if r < rows - 1 else late_c.at[0]
+                return pltpu.make_async_copy(kvbuf.at[(r // 2) % 2, r % 2], target_ref, late_sem.at[1, r])
 
             for r in range(rows):
                 if r >= 4:
@@ -440,9 +496,21 @@
 
         @pl.when(me == target)
         def _():
-            copy = pltpu.make_async_copy(late, out.at[pl.ds(ROWS - rows, rows), 0, pl.ds((target + 2) * BLOCK, BLOCK)], sem)
+            place = out.at[pl.ds(ROWS - rows, rows - 1), 0, pl.ds((target + 2) * BLOCK, BLOCK)]
+            copy = pltpu.make_async_copy(late, place, sem)
             copy.start()
             copy.wait()
+
+
+def last_kernel(late_c, old, out, sem):
+    me = lax.axis_index("a")
+
+    @pl.when(me < 2)
+    def _():
+        place = pl.multiple_of((me + 2) * BLOCK, BLOCK)
+        copy = pltpu.make_async_copy(late_c, out.at[pl.ds(ROWS - 1, 1), 0, pl.ds(place, BLOCK)], sem)
+        copy.start()
+        copy.wait()
 
 
 def trig_table():
@@ -473,9 +541,10 @@
             move_kernel,
             out_shape=(loc_land, loc_land, glo_land, glo_land,
                        jax.ShapeDtypeStruct((ROWS, model), bf16), jax.ShapeDtypeStruct((4, ROWS, HEAD), bf16),
-                       jax.ShapeDtypeStruct((LATE[0], BLOCK, HEAD), bf16), jax.ShapeDtypeStruct((LATE[1], BLOCK, HEAD), bf16)),
+                       jax.ShapeDtypeStruct((LATE[0] - 1, BLOCK, HEAD), bf16),
+                       jax.ShapeDtypeStruct((LATE[1] - 1, BLOCK, HEAD), bf16), jax.ShapeDtypeStruct((1, BLOCK, HEAD), bf16)),
             in_specs=[anywhere] * 18,
-            out_specs=(anywhere,) * 8,
+            out_specs=(anywhere,) * 9,
             scratch_shapes=[
                 pltpu.VMEM((ROWS, model), bf16), pltpu.VMEM((2, HEAD // 2), f32),
                 pltpu.VMEM((model,), bf16), pltpu.VMEM((model,), bf16), pltpu.VMEM((model,), bf16), pltpu.VMEM((model,), bf16),
@@ -485,18 +554,20 @@
                 pltpu.VMEM((2, 2, BLOCK, HEAD), bf16),
                 pltpu.VMEM((2, GROUP, 2 * ROWS, HEAD), bf16),
                 pltpu.VMEM((2, GROUP, 2 * ROWS, HEAD + 2 * STAT), f32),
-                pltpu.VMEM((2, 3, 2 * ROWS, HEAD + 2 * STAT), f32),
-                pltpu.VMEM((2, 2 * ROWS, HEAD + 2 * STAT), f32),
+                pltpu.VMEM((2, 4, 2 * ROWS, HEAD + 2 * STAT), f32),
+                pltpu.VMEM((2, 2, 2 * ROWS, HEAD + 2 * STAT), f32),
+                pltpu.VMEM((2, 2, 2 * ROWS, HEAD), bf16),
                 pltpu.VMEM((2, GROUP, ROWS, model), bf16), pltpu.VMEM((2, 2, ROWS, model // 2), bf16),
                 dma((3, DEPTH)), dma((2, LOC_UNITS)), dma((2, GLO_UNITS)), dma((8,)), dma((2, 2)),
-                dma((22,)), dma((22,)), dma((2, LATE[0])),
-                dma((LATE[0] - LATE[1], PER)), dma((6,)), dma((2,))],
+                dma((26,)), dma((26,)), dma((2, LATE[0])),
+                dma((LATE[0] - LATE[1], PER)), dma((6,)), dma((2,)), dma((2,))],
             compiler_params=pltpu.CompilerParams(collective_id=0, has_side_effects=True),
         )(hidden_in, jnp.asarray(trig_table()), *gains, loc_k, loc_v, glo_k, glo_v,
           loc_wq, loc_wk, loc_wv, loc_wo, glo_wq, glo_wk, glo_wv, glo_wo)
         land, hid, new_kv = moved[:4], moved[4], moved[5]
         late_a = lax.ppermute(moved[6], 'a', [(2, 0)])
         late_b = lax.ppermute(moved[7], 'a', [(3, 1)])
+        late_c = lax.ppermute(moved[8], 'a', [(2, 0), (3, 1)])
         hidden_out, loc_k_out, loc_v_out, glo_k_out, glo_v_out = pl.pallas_call(
             write_kernel,
             out_shape=(jax.ShapeDtypeStruct((ROWS, model), bf16),)
@@ -518,6 +589,16 @@
             compiler_params=pltpu.CompilerParams(vmem_limit_bytes=16 * 2 ** 20),
             cost_estimate=pl.CostEstimate(flops=10 ** 7, bytes_accessed=4 * late_a.size, transcendentals=0),
         )(late_a, late_b, glo_v_out)
+        glo_v_out = pl.pallas_call(
+            last_kernel,
+            out_shape=jax.ShapeDtypeStruct(glo_v_out.shape, bf16),
+            in_specs=[vmem, anywhere],
+            out_specs=anywhere,
+            scratch_shapes=[dma],
+            input_output_aliases={1: 0},
+            compiler_params=pltpu.CompilerParams(vmem_limit_bytes=16 * 2 ** 20),
+            cost_estimate=pl.CostEstimate(flops=10 ** 6, bytes_accessed=4 * late_c.size, transcendentals=0),
+        )(late_c, glo_v_out)
         return hidden_out, loc_k_out, loc_v_out, glo_k_out, glo_v_out
 
     return jax.shard_map(device_step, mesh=mesh, in_specs=in_specs, out_specs=out_specs, check_vma=False)

time: 1090 us -> 1090 us (level)
    ppermute x1, waiting for transfers between devices: 22.7 us -> 4.57 us  [device_step(): late_a = lax.ppermute(moved[6], 'a', [(2, 0)])]
    ppermute x0 -> x1, waiting for transfers between devices: none -> 15.2 us  [device_step(): late_c = lax.ppermute(moved[8], 'a', [(2, 0), (3, 1)])]
  transfers between devices with their start and end apart: 2 -> 3, of which waited for: 1 -> 2; matrix products, arithmetic and copies ran while one was open for 0% -> 0% of each run, Pallas kernels for 5% -> 5%
where the time goes in v5:
time: 1090 us
  Pallas kernels  1060 us (97%)
  waiting for transfers between devices  19.7 us (2%)
    pallas_call x1, Pallas kernels, device_step(): pl.pallas_call(move_kernel, out_shape=(loc_land, loc_land, glo_land, glo_...  1000 us
    pallas_call x1, Pallas kernels, device_step(): pl.pallas_call(write_kernel, out_shape=(jax.ShapeDtypeStruct((ROWS, model...  56.7 us
  transfers between devices with their start and end apart: 3, of which 2 were waited for; matrix products, arithmetic and copies ran while one was open for 0% of the time, Pallas kernels for 5%

profile of v5, /device:TPU:0, one launch (start us, length us, event | category | flops | bytes accessed | tf_op | source)
XLA Modules:
  0.0 1085.8 jit_solution(4762284757292829100)
XLA Ops:
  0.6 1001.3 %shard_map.209 = (bf16[8,1,4096,256]{3,2,1,0:T(8,128)(2,1)}, bf16[8,1,4096,256]{3,2,1,0:T(8,128)(2,1)}, bf16[8,1,6144,256]{3,2,1,0:T(8,128)(2,1)}, bf16[8,1,6144...) custom-call(bf16[8,2560]{1,0:T(8,128)(2,1)} %hid_in.1, ...), custom_call_target="tpu_custom_call" | custom-call | tf_op jit(solution)/shard_map/pallas_call | solution.py:540
  1001.9 1.3 collective-permute-start.1
  1003.2 0.8 collective-permute-start.2
  1004.0 1.3 collective-permute-start
  1005.3 0.0 copy-start
  1005.3 0.8 copy-done
  1006.1 0.0 copy-start.1
  1006.1 0.7 copy-done.1
  1006.8 56.7 %shard_map.210 = (bf16[8,2560]{1,0:T(8,128)(2,1)}, bf16[8,1,4096,256]{3,2,1,0:T(8,128)(2,1)}, bf16[8,1,4096,256]{3,2,1,0:T(8,128)(2,1)}, bf16[8,1,6656,256]{3,2,1,0:T(8,128)(2,1)}, bf16[8,1,6656,256]{3,2,1,0:T(8,128)(2,1)}) custom-call(bf16[8,2560]{1,0:T(8,128)(2,1)S(1)} %copy-done, bf16[4,8,256]{2,1,0:T(8,128)(2,1)S(1)} %copy-done.1, ...), custom_call_target="tpu_custom_call" | custom-call | flops 1000000000 | bytes 180000000 | tf_op jit(solution)/shard_map/pallas_call | solution.py:571
  1063.5 0.0 collective-permute-done.2.late_b
  1063.5 4.6 collective-permute-done.1.late_a
  1068.1 1.7 shard_map.211.old
  1069.8 15.2 %collective-permute-done.late_c = bf16[1,1536,256]{2,1,0:T(8,128)(2,1)S(1)} collective-permute-done((bf16[1,1536,256]{2,1,0:T(8,128)(2,1)}, bf16[1,1536,256]{2,1,0:T(8,128)(2,1)S(1)}, u32[]{:S(2)}, u32[]{:S(2)}) %collective-permute-start) | collective-permute-done | bytes 786464 | tf_op jit(solution)/shard_map/ppermute | solution.py:570
  1085.0 0.9 shard_map.212
Async XLA Ops:
  1001.9 66.2 %collective-permute-start.1 = (bf16[4,1536,256]{2,1,0:T(8,128)(2,1)}, bf16[4,1536,256]{2,1,0:T(8,128)(2,1)S(1)}, u32[]{:S(2)}, u32[]{:S(2)}) collective-permute-start(bf16[4,1536,256]{2,1,0:T(8,128)(2,1)} %get-tuple-element.30), channel_id=1, source_target_pairs={{2,0},{6,4}} | collective-permute-start | bytes 9437192 | tf_op jit(solution)/shard_map/ppermute | solution.py:568
  1003.2 60.3 %collective-permute-start.2 = (bf16[3,1536,256]{2,1,0:T(8,128)(2,1)}, bf16[3,1536,256]{2,1,0:T(8,128)(2,1)S(1)}, u32[]{:S(2)}, u32[]{:S(2)}) collective-permute-start(bf16[3,1536,256]{2,1,0:T(8,128)(2,1)} %get-tuple-element.31), channel_id=1, source_target_pairs={{3,1},{7,5}} | collective-permute-start | bytes 7077896 | tf_op jit(solution)/shard_map/ppermute | solution.py:569
  1004.0 80.9 %collective-permute-start = (bf16[1,1536,256]{2,1,0:T(8,128)(2,1)}, bf16[1,1536,256]{2,1,0:T(8,128)(2,1)S(1)}, u32[]{:S(2)}, u32[]{:S(2)}) collective-permute-start(bf16[1,1536,256]{2,1,0:T(8,128)(2,1)} %get-tuple-element.29), channel_id=1, source_target_pairs={{2,0},{3,1},{6,4},{7,5}} | collective-permute-start | bytes 2359304 | tf_op jit(solution)/shard_map/ppermute | solution.py:570
  1005.3 0.8 copy-start
  1006.1 0.7 copy-start.1

commit v6 on v5

--- a/solution.py
+++ b/solution.py
@@ -26,6 +26,8 @@
 DEPTH = 2
 LATE = (5, 4)
 MESH = pl.DeviceIdType.MESH
+PIECES = 8
+WO_ROWS = 64
 STAT = 64
 LOW = -1e30
 
@@ -45,8 +47,8 @@
 
 def move_kernel(hid_in, trig_in, lpre_in, lpost_in, gpre_in, gpost_in, lk, lv, gk, gv, lwq, lwk, lwv, lwo, gwq, gwk, gwv, gwo,
                 land_lk, land_lv, land_gk, land_gv, hid_out, new_out, late_a, late_b, late_c,
-                hid, trig, lpre, lpost, gpre, gpost, new_kv, hid_end, wq, wk, wv, wo, kvbuf, qbuf, part, precv, pair, att, ybuf, hbuf,
-                bulk_send, loc_recv, glo_recv, w_sem, kv_sem, ex_send, ex_recv, late_sem, tail_send, small_sem, out_sem, first_sem):
+                hid, trig, lpre, lpost, gpre, gpost, new_kv, hid_end, wq, wk, wv, wo, kvbuf, qbuf, part, precv, pair, att, ybuf, hbuf, wo_far,
+                bulk_send, loc_recv, glo_recv, w_sem, kv_sem, ex_send, ex_recv, late_sem, tail_send, small_sem, out_sem, first_sem, wo_send, wo_recv):
     dp = lax.axis_index("dp")
     me = lax.axis_index("a")
     dest = peers(me)
@@ -67,7 +69,7 @@
     pl.semaphore_wait(barrier, 3)
 
     def coords(step):
-        c = (step // (ROWS * PER) + 2 - 2 * (me // 2)) % 4
+        c = step // (ROWS * PER) * (3 - 2 * (me // 2)) % 4
         return c, (step // PER) % ROWS, step % PER
 
     def valid(step, k):
@@ -89,6 +91,23 @@
                     src_ref=gk.at[0, 0, pl.ds(0, UNIT)], dst_ref=land_gk.at[0, 0, pl.ds(0, UNIT)],
                     send_sem=bulk_send.at[k, slot], recv_sem=glo_recv.at[0, 0],
                     device_id=(dp, dest[k]), device_id_type=MESH).wait_send()
+        def piece(s, ref):
+            rows = pl.ds(pl.multiple_of(s % PIECES * WO_ROWS, WO_ROWS), WO_ROWS)
+            return pltpu.make_async_remote_copy(
+                src_ref=ref.at[rows], dst_ref=wo_far.at[s // PIECES, rows], send_sem=wo_send.at[s % DEPTH],
+                recv_sem=wo_recv.at[s // PIECES], device_id=(dp, dest[1]), device_id_type=MESH)
+
+        before = step - DEPTH
+
+        @pl.when(jnp.logical_and(me < 2, jnp.logical_and(before >= 0, before < 2 * PIECES)))
+        def _():
+            piece(before, lwo).wait_send()
+
+        for i, ref in enumerate((lwo, gwo)):
+            @pl.when(jnp.logical_and(me < 2, jnp.logical_and(step >= i * PIECES, step < (i + 1) * PIECES)))
+            def _():
+                piece(step, ref).start()
+
         unit = PER * me + j
         for i in range(4):
             place = unit % LOC_UNITS if i < 2 else unit
@@ -159,7 +178,7 @@
         new_kv[2 * index + 1] = new_v
         own_q = qbuf.at[index]
         own_q[me] = q
-        base = 11 * index
+        base = 8 * index
         near = send(base, 0, own_q.at[me], own_q.at[me])
         far = send(base + 1, 1, own_q.at[me], own_q.at[me])
         near.start()
@@ -248,9 +267,14 @@
         across = pair.at[index]
         across[0] = packed(*merge([split(mine[dest[1]]), split(theirs[1])]))
         across[1] = packed(*merge(both))
-        result = att.at[index]
+        heads = att.at[index]
         far = [send(base + 5 + i, 1, across.at[i], theirs.at[2 + i]) for i in (0, 1)]
-        reply = send(base + 7, 1, result.at[1], result.at[0])
+        y_ref = ybuf.at[index]
+        half = hbuf.at[index]
+        side = me % 2
+        near = send(base + 7, 0, y_ref.at[side], y_ref.at[side])
+        back = send(16 + 2 * index, 1, half.at[side], half.at[side])
+        swap = send(17 + 2 * index, 0, half.at[side], half.at[side])
 
         @pl.when(me < 2)
         def _():
@@ -263,57 +287,27 @@
         def _():
             for copy in far:
                 copy.wait_recv()
-            acc, _, total = merge(both + [split(theirs[2])])
-            result[0] = (acc / total).astype(jnp.bfloat16)
-            acc, _, total = merge([split(across[0]), split(theirs[3])])
-            result[1] = (acc / total).astype(jnp.bfloat16)
-            reply.start()
+
+            def finished(blocks):
+                acc, _, total = merge(blocks)
+                out = (acc / total).astype(jnp.bfloat16)
+                return jnp.concatenate([out[:ROWS], out[ROWS:]], axis=-1)
+
+            heads[0] = finished(both + [split(theirs[2])])
+            heads[1] = finished([split(across[0]), split(theirs[3])])
 
         pump(step + 1)
 
         @pl.when(me >= 2)
         def _():
-            reply.wait_send()
-
-        @pl.when(me < 2)
-        def _():
-            for copy in far:
-                copy.wait_send()
-            reply.wait_recv()
-
-        heads = result[0]
-        step = step + 1
-        own = jnp.concatenate([heads[:ROWS], heads[ROWS:]], axis=-1)
-        y = jnp.dot(own, wo[index], preferred_element_type=jnp.float32).astype(jnp.bfloat16)
-        y_ref = ybuf.at[index]
-        y_ref[me] = y
-        near = send(base + 8, 0, y_ref.at[me], y_ref.at[me])
-        far = [send(base + 8 + k, k, y_ref.at[me], y_ref.at[me]) for k in (1, 2)]
-        half = hbuf.at[index]
-        side = me % 2
-        back = send(22 + 2 * index, 1, half.at[side], half.at[side])
-        swap = send(23 + 2 * index, 0, half.at[side], half.at[side])
-
-        @pl.when(me >= 2)
-        def _():
+            pltpu.make_async_remote_copy(
+                src_ref=wo_far.at[index], dst_ref=wo_far.at[index], send_sem=wo_send.at[0], recv_sem=wo_recv.at[index],
+                device_id=(dp, dest[1]), device_id_type=MESH).wait_recv()
+            y_ref[side] = (jnp.dot(heads[0], wo[index], preferred_element_type=jnp.float32)
+                           + jnp.dot(heads[1], wo_far[index], preferred_element_type=jnp.float32))
             near.start()
-
-        @pl.when(me < 2)
-        def _():
-            for copy in far:
-                copy.start()
-
-        pump(step + 1)
-
-        @pl.when(me >= 2)
-        def _():
-            near.wait_recv()
-            for copy in far:
-                copy.wait_recv()
-            summed = y_ref[0].astype(jnp.float32)
-            for d in range(1, GROUP):
-                summed = summed + y_ref[d].astype(jnp.float32)
-            after = (hidden + norm(summed, post[...])).astype(jnp.bfloat16)
+            near.wait()
+            after = (hidden + norm(y_ref[0] + y_ref[1], post[...])).astype(jnp.bfloat16)
             half[0] = after[:, :after.shape[1] // 2]
             half[1] = after[:, after.shape[1] // 2:]
             back.start()
@@ -322,7 +316,6 @@
 
         @pl.when(me >= 2)
         def _():
-            near.wait_send()
             back.wait_send()
 
         @pl.when(me < 2)
@@ -352,9 +345,11 @@
                 return pltpu.make_async_copy(gv.at[ROWS - rows + r, target], kvbuf.at[(r // 2) % 2, r % 2], late_sem.at[0, r])
 
             def late_out(r):
-                target_ref = late.at[r] if r < rows - 1 else late_c.at[0]
-                return pltpu.make_async_copy(kvbuf.at[(r // 2) % 2, r % 2], target_ref, late_sem.at[1, r])
-
+                buf, size = kvbuf.at[(r // 2) % 2, r % 2], BLOCK if r < rows - 1 else BLOCK - UNIT
+                return pltpu.make_async_copy(buf.at[pl.ds(0, size)], late.at[pl.ds(r * BLOCK, size)], late_sem.at[1, r])
+
+            end = kvbuf.at[((rows - 1) // 2) % 2, (rows - 1) % 2, pl.ds(BLOCK - UNIT, UNIT)]
+            last_out = pltpu.make_async_copy(end, late_c, late_sem.at[0, rows - 1])
             for r in range(rows):
                 if r >= 4:
                     late_out(r - 4).wait()
@@ -364,8 +359,10 @@
                     late_out(r - 1).start()
             late_in(rows - 1).wait()
             late_out(rows - 1).start()
+            last_out.start()
             for r in range(max(rows - 4, 0), rows):
                 late_out(r).wait()
+            last_out.wait()
 
     def rest(s, carry):
         pump(s)
@@ -492,14 +489,18 @@
 def late_kernel(late_a, late_b, old, out, sem):
     me = lax.axis_index("a")
     for target, late in enumerate((late_a, late_b)):
-        rows = LATE[target]
-
         @pl.when(me == target)
         def _():
-            place = out.at[pl.ds(ROWS - rows, rows - 1), 0, pl.ds((target + 2) * BLOCK, BLOCK)]
-            copy = pltpu.make_async_copy(late, place, sem)
-            copy.start()
-            copy.wait()
+            copies = []
+            for r in range(LATE[target]):
+                size = BLOCK if r < LATE[target] - 1 else BLOCK - UNIT
+                copies.append(pltpu.make_async_copy(
+                    late.at[pl.ds(r * BLOCK, size)],
+                    out.at[ROWS - LATE[target] + r, 0, pl.ds((target + 2) * BLOCK, size)], sem.at[r]))
+            for copy in copies:
+                copy.start()
+            for copy in copies:
+                copy.wait()
 
 
 def last_kernel(late_c, old, out, sem):
@@ -507,8 +508,8 @@
 
     @pl.when(me < 2)
     def _():
-        place = pl.multiple_of((me + 2) * BLOCK, BLOCK)
-        copy = pltpu.make_async_copy(late_c, out.at[pl.ds(ROWS - 1, 1), 0, pl.ds(place, BLOCK)], sem)
+        place = pl.multiple_of((me + 3) * BLOCK - UNIT, UNIT)
+        copy = pltpu.make_async_copy(late_c, out.at[ROWS - 1, 0, pl.ds(place, UNIT)], sem)
         copy.start()
         copy.wait()
 
@@ -541,8 +542,8 @@
             move_kernel,
             out_shape=(loc_land, loc_land, glo_land, glo_land,
                        jax.ShapeDtypeStruct((ROWS, model), bf16), jax.ShapeDtypeStruct((4, ROWS, HEAD), bf16),
-                       jax.ShapeDtypeStruct((LATE[0] - 1, BLOCK, HEAD), bf16),
-                       jax.ShapeDtypeStruct((LATE[1] - 1, BLOCK, HEAD), bf16), jax.ShapeDtypeStruct((1, BLOCK, HEAD), bf16)),
+                       jax.ShapeDtypeStruct((LATE[0] * BLOCK - UNIT, HEAD), bf16),
+                       jax.ShapeDtypeStruct((LATE[1] * BLOCK - UNIT, HEAD), bf16), jax.ShapeDtypeStruct((UNIT, HEAD), bf16)),
             in_specs=[anywhere] * 18,
             out_specs=(anywhere,) * 9,
             scratch_shapes=[
@@ -556,11 +557,12 @@
                 pltpu.VMEM((2, GROUP, 2 * ROWS, HEAD + 2 * STAT), f32),
                 pltpu.VMEM((2, 4, 2 * ROWS, HEAD + 2 * STAT), f32),
                 pltpu.VMEM((2, 2, 2 * ROWS, HEAD + 2 * STAT), f32),
-                pltpu.VMEM((2, 2, 2 * ROWS, HEAD), bf16),
-                pltpu.VMEM((2, GROUP, ROWS, model), bf16), pltpu.VMEM((2, 2, ROWS, model // 2), bf16),
+                pltpu.VMEM((2, 2, ROWS, 2 * HEAD), bf16),
+                pltpu.VMEM((2, 2, ROWS, model), f32), pltpu.VMEM((2, 2, ROWS, model // 2), bf16),
+                pltpu.VMEM((2,) + loc_wo.shape, bf16),
                 dma((3, DEPTH)), dma((2, LOC_UNITS)), dma((2, GLO_UNITS)), dma((8,)), dma((2, 2)),
-                dma((26,)), dma((26,)), dma((2, LATE[0])),
-                dma((LATE[0] - LATE[1], PER)), dma((6,)), dma((2,)), dma((2,))],
+                dma((20,)), dma((20,)), dma((2, LATE[0])),
+                dma((LATE[0] - LATE[1], PER)), dma((6,)), dma((2,)), dma((2,)), dma((DEPTH,)), dma((2,))],
             compiler_params=pltpu.CompilerParams(collective_id=0, has_side_effects=True),
         )(hidden_in, jnp.asarray(trig_table()), *gains, loc_k, loc_v, glo_k, glo_v,
           loc_wq, loc_wk, loc_wv, loc_wo, glo_wq, glo_wk, glo_wv, glo_wo)
@@ -584,7 +586,7 @@
             out_shape=jax.ShapeDtypeStruct(glo_v_out.shape, bf16),
             in_specs=[vmem, vmem, anywhere],
             out_specs=anywhere,
-            scratch_shapes=[dma],
+            scratch_shapes=[dma((LATE[0],))],
             input_output_aliases={2: 0},
             compiler_params=pltpu.CompilerParams(vmem_limit_bytes=16 * 2 ** 20),
             cost_estimate=pl.CostEstimate(flops=10 ** 7, bytes_accessed=4 * late_a.size, transcendentals=0),

time: 1090 us -> 1090 us (level)
    ppermute x1, waiting for transfers between devices: 15.2 us -> 3.74 us  [device_step(): late_c = lax.ppermute(moved[8], 'a', [(2, 0), (3, 1)])]
    ppermute x1, waiting for transfers between devices: 4.57 us -> 15.8 us  [device_step(): late_a = lax.ppermute(moved[6], 'a', [(2, 0)])]
where the time goes in v6:
time: 1090 us
  Pallas kernels  1060 us (97%)
  waiting for transfers between devices  19.5 us (2%)
    pallas_call x1, Pallas kernels, device_step(): pl.pallas_call(move_kernel, out_shape=(loc_land, loc_land, glo_land, glo_...  1000 us
    pallas_call x1, Pallas kernels, device_step(): pl.pallas_call(write_kernel, out_shape=(jax.ShapeDtypeStruct((ROWS, model...  56.7 us
  transfers between devices with their start and end apart: 3, of which 2 were waited for; matrix products, arithmetic and copies ran while one was open for 0% of the time, Pallas kernels for 5%

profile of v6, /device:TPU:0, one launch (start us, length us, event | category | flops | bytes accessed | tf_op | source)
XLA Modules:
  0.0 1085.3 jit_solution(12626636258280251565)
XLA Ops:
  0.6 1000.8 %shard_map.209 = (bf16[8,1,4096,256]{3,2,1,0:T(8,128)(2,1)}, bf16[8,1,4096,256]{3,2,1,0:T(8,128)(2,1)}, bf16[8,1,6144,256]{3,2,1,0:T(8,128)(2,1)}, bf16[8,1,6144...) custom-call(bf16[8,2560]{1,0:T(8,128)(2,1)} %hid_in.1, ...), custom_call_target="tpu_custom_call" | custom-call | tf_op jit(solution)/shard_map/pallas_call | solution.py:541
  1001.5 1.3 collective-permute-start.1
  1002.8 0.8 collective-permute-start.2
  1003.6 1.3 collective-permute-start
  1004.9 0.0 copy-start
  1004.9 0.8 copy-done
  1005.7 0.0 copy-start.1
  1005.7 0.7 copy-done.1
  1006.4 56.7 %shard_map.210 = (bf16[8,2560]{1,0:T(8,128)(2,1)}, bf16[8,1,4096,256]{3,2,1,0:T(8,128)(2,1)}, bf16[8,1,4096,256]{3,2,1,0:T(8,128)(2,1)}, bf16[8,1,6656,256]{3,2,1,0:T(8,128)(2,1)}, bf16[8,1,6656,256]{3,2,1,0:T(8,128)(2,1)}) custom-call(bf16[8,2560]{1,0:T(8,128)(2,1)S(1)} %copy-done, bf16[4,8,256]{2,1,0:T(8,128)(2,1)S(1)} %copy-done.1, ...), custom_call_target="tpu_custom_call" | custom-call | flops 1000000000 | bytes 180000000 | tf_op jit(solution)/shard_map/pallas_call | solution.py:573
  1063.1 0.0 collective-permute-done.2.late_b
  1063.1 15.8 %collective-permute-done.1.late_a = bf16[7168,256]{1,0:T(8,128)(2,1)S(1)} collective-permute-done((bf16[7168,256]{1,0:T(8,128)(2,1)}, bf16[7168,256]{1,0:T(8,128)(2,1)S(1)}, u32[]{:S(2)}, u32[]{:S(2)}) %collective-permute-start.1) | collective-permute-done | bytes 3670048 | tf_op jit(solution)/shard_map/ppermute | solution.py:570
  1078.9 1.9 shard_map.211.old
  1080.8 3.7 collective-permute-done.late_c
  1084.6 0.7 shard_map.212
Async XLA Ops:
  1001.5 77.5 %collective-permute-start.1 = (bf16[7168,256]{1,0:T(8,128)(2,1)}, bf16[7168,256]{1,0:T(8,128)(2,1)S(1)}, u32[]{:S(2)}, u32[]{:S(2)}) collective-permute-start(bf16[7168,256]{1,0:T(8,128)(2,1)} %get-tuple-element.30), channel_id=1, source_target_pairs={{2,0},{6,4}} | collective-permute-start | bytes 11010056 | tf_op jit(solution)/shard_map/ppermute | solution.py:570
  1002.8 60.4 %collective-permute-start.2 = (bf16[5632,256]{1,0:T(8,128)(2,1)}, bf16[5632,256]{1,0:T(8,128)(2,1)S(1)}, u32[]{:S(2)}, u32[]{:S(2)}) collective-permute-start(bf16[5632,256]{1,0:T(8,128)(2,1)} %get-tuple-element.31), channel_id=1, source_target_pairs={{3,1},{7,5}} | collective-permute-start | bytes 8650760 | tf_op jit(solution)/shard_map/ppermute | solution.py:571
  1003.6 80.9 %collective-permute-start = (bf16[512,256]{1,0:T(8,128)(2,1)}, bf16[512,256]{1,0:T(8,128)(2,1)S(1)}, u32[]{:S(2)}, u32[]{:S(2)}) collective-permute-start(bf16[512,256]{1,0:T(8,128)(2,1)} %get-tuple-element.29), channel_id=1, source_target_pairs={{2,0},{3,1},{6,4},{7,5}} | collective-permute-start | bytes 786440 | tf_op jit(solution)/shard_map/ppermute | solution.py:572
  1004.9 0.8 copy-start
  1005.7 0.7 copy-start.1

commit v7 on v6

--- a/solution.py
+++ b/solution.py
@@ -28,6 +28,8 @@
 MESH = pl.DeviceIdType.MESH
 PIECES = 8
 WO_ROWS = 64
+LAST = 256
+FIRST = 16
 STAT = 64
 LOW = -1e30
 
@@ -55,7 +57,7 @@
     caches = (lk, lv, gk, gv)
     lands = (land_lk, land_lv, land_gk, land_gv)
 
-    first = [pltpu.make_async_copy(lk.at[0, dest[k], pl.ds(0, UNIT)], kvbuf.at[0, k - 1, pl.ds(0, UNIT)], first_sem.at[k - 1])
+    first = [pltpu.make_async_copy(lk.at[0, dest[k], pl.ds(0, FIRST)], kvbuf.at[0, k - 1, pl.ds(0, FIRST)], first_sem.at[k - 1])
              for k in (1, 2)]
 
     @pl.when(me >= 2)
@@ -144,8 +146,13 @@
         for k in (1, 2):
             first[k - 1].wait()
             pltpu.make_async_remote_copy(
-                src_ref=kvbuf.at[0, k - 1, pl.ds(0, UNIT)],
-                dst_ref=land_lk.at[0, 0, pl.ds(pl.multiple_of(place * UNIT, UNIT), UNIT)],
+                src_ref=kvbuf.at[0, k - 1, pl.ds(0, FIRST)],
+                dst_ref=land_lk.at[0, 0, pl.ds(pl.multiple_of(place * UNIT, UNIT), FIRST)],
+                send_sem=bulk_send.at[k, 0], recv_sem=loc_recv.at[0, place],
+                device_id=(dp, dest[k]), device_id_type=MESH).start()
+            pltpu.make_async_remote_copy(
+                src_ref=lk.at[0, dest[k], pl.ds(FIRST, UNIT - FIRST)],
+                dst_ref=land_lk.at[0, 0, pl.ds(pl.multiple_of(place * UNIT + FIRST, FIRST), UNIT - FIRST)],
                 send_sem=bulk_send.at[k, 0], recv_sem=loc_recv.at[0, place],
                 device_id=(dp, dest[k]), device_id_type=MESH).start()
 
@@ -345,10 +352,10 @@
                 return pltpu.make_async_copy(gv.at[ROWS - rows + r, target], kvbuf.at[(r // 2) % 2, r % 2], late_sem.at[0, r])
 
             def late_out(r):
-                buf, size = kvbuf.at[(r // 2) % 2, r % 2], BLOCK if r < rows - 1 else BLOCK - UNIT
+                buf, size = kvbuf.at[(r // 2) % 2, r % 2], BLOCK if r < rows - 1 else BLOCK - LAST
                 return pltpu.make_async_copy(buf.at[pl.ds(0, size)], late.at[pl.ds(r * BLOCK, size)], late_sem.at[1, r])
 
-            end = kvbuf.at[((rows - 1) // 2) % 2, (rows - 1) % 2, pl.ds(BLOCK - UNIT, UNIT)]
+            end = kvbuf.at[((rows - 1) // 2) % 2, (rows - 1) % 2, pl.ds(BLOCK - LAST, LAST)]
             last_out = pltpu.make_async_copy(end, late_c, late_sem.at[0, rows - 1])
             for r in range(rows):
                 if r >= 4:
@@ -493,7 +500,7 @@
         def _():
             copies = []
             for r in range(LATE[target]):
-                size = BLOCK if r < LATE[target] - 1 else BLOCK - UNIT
+                size = BLOCK if r < LATE[target] - 1 else BLOCK - LAST
                 copies.append(pltpu.make_async_copy(
                     late.at[pl.ds(r * BLOCK, size)],
                     out.at[ROWS - LATE[target] + r, 0, pl.ds((target + 2) * BLOCK, size)], sem.at[r]))
@@ -508,8 +515,8 @@
 
     @pl.when(me < 2)
     def _():
-        place = pl.multiple_of((me + 3) * BLOCK - UNIT, UNIT)
-        copy = pltpu.make_async_copy(late_c, out.at[ROWS - 1, 0, pl.ds(place, UNIT)], sem)
+        place = pl.multiple_of((me + 3) * BLOCK - LAST, LAST)
+        copy = pltpu.make_async_copy(late_c, out.at[ROWS - 1, 0, pl.ds(place, LAST)], sem)
         copy.start()
         copy.wait()
 
@@ -542,8 +549,8 @@
             move_kernel,
             out_shape=(loc_land, loc_land, glo_land, glo_land,
                        jax.ShapeDtypeStruct((ROWS, model), bf16), jax.ShapeDtypeStruct((4, ROWS, HEAD), bf16),
-                       jax.ShapeDtypeStruct((LATE[0] * BLOCK - UNIT, HEAD), bf16),
-                       jax.ShapeDtypeStruct((LATE[1] * BLOCK - UNIT, HEAD), bf16), jax.ShapeDtypeStruct((UNIT, HEAD), bf16)),
+                       jax.ShapeDtypeStruct((LATE[0] * BLOCK - LAST, HEAD), bf16),
+                       jax.ShapeDtypeStruct((LATE[1] * BLOCK - LAST, HEAD), bf16), jax.ShapeDtypeStruct((LAST, HEAD), bf16)),
             in_specs=[anywhere] * 18,
             out_specs=(anywhere,) * 9,
             scratch_shapes=[

time: 1090 us -> 1090 us (level)
  no operation moved by 1% of the time
where the time goes in v7:
time: 1090 us; the launch traced here: 1080 us
  Pallas kernels  1060 us (97%)
  waiting for transfers between devices  19.5 us (2%)
    pallas_call x1, Pallas kernels, device_step(): pl.pallas_call(move_kernel, out_shape=(loc_land, loc_land, glo_land, glo_...  1000 us
    pallas_call x1, Pallas kernels, device_step(): pl.pallas_call(write_kernel, out_shape=(jax.ShapeDtypeStruct((ROWS, model...  56.7 us
  transfers between devices with their start and end apart: 3, of which 2 were waited for; matrix products, arithmetic and copies ran while one was open for 0% of the time, Pallas kernels for 5%

profile of v7, /device:TPU:0, one launch (start us, length us, event | category | flops | bytes accessed | tf_op | source)
XLA Modules:
  0.0 1085.0 jit_solution(14421749145645230062)
XLA Ops:
  0.6 1000.6 %shard_map.209 = (bf16[8,1,4096,256]{3,2,1,0:T(8,128)(2,1)}, bf16[8,1,4096,256]{3,2,1,0:T(8,128)(2,1)}, bf16[8,1,6144,256]{3,2,1,0:T(8,128)(2,1)}, bf16[8,1,6144...) custom-call(bf16[8,2560]{1,0:T(8,128)(2,1)} %hid_in.1, ...), custom_call_target="tpu_custom_call" | custom-call | tf_op jit(solution)/shard_map/pallas_call | solution.py:548
  1001.2 1.3 collective-permute-start.1
  1002.5 0.9 collective-permute-start.2
  1003.4 1.3 collective-permute-start
  1004.7 0.0 copy-start
  1004.7 0.8 copy-done
  1005.5 0.0 copy-start.1
  1005.5 0.7 copy-done.1
  1006.2 56.7 %shard_map.210 = (bf16[8,2560]{1,0:T(8,128)(2,1)}, bf16[8,1,4096,256]{3,2,1,0:T(8,128)(2,1)}, bf16[8,1,4096,256]{3,2,1,0:T(8,128)(2,1)}, bf16[8,1,6656,256]{3,2,1,0:T(8,128)(2,1)}, bf16[8,1,6656,256]{3,2,1,0:T(8,128)(2,1)}) custom-call(bf16[8,2560]{1,0:T(8,128)(2,1)S(1)} %copy-done, bf16[4,8,256]{2,1,0:T(8,128)(2,1)S(1)} %copy-done.1, ...), custom_call_target="tpu_custom_call" | custom-call | flops 1000000000 | bytes 180000000 | tf_op jit(solution)/shard_map/pallas_call | solution.py:580
  1062.9 0.0 collective-permute-done.2.late_b
  1062.9 18.6 %collective-permute-done.1.late_a = bf16[7424,256]{1,0:T(8,128)(2,1)S(1)} collective-permute-done((bf16[7424,256]{1,0:T(8,128)(2,1)}, bf16[7424,256]{1,0:T(8,128)(2,1)S(1)}, u32[]{:S(2)}, u32[]{:S(2)}) %collective-permute-start.1) | collective-permute-done | bytes 3801120 | tf_op jit(solution)/shard_map/ppermute | solution.py:577
  1081.5 1.9 shard_map.211.old
  1083.4 0.9 collective-permute-done.late_c
  1084.3 0.7 shard_map.212
Async XLA Ops:
  1001.2 80.3 %collective-permute-start.1 = (bf16[7424,256]{1,0:T(8,128)(2,1)}, bf16[7424,256]{1,0:T(8,128)(2,1)S(1)}, u32[]{:S(2)}, u32[]{:S(2)}) collective-permute-start(bf16[7424,256]{1,0:T(8,128)(2,1)} %get-tuple-element.30), channel_id=1, source_target_pairs={{2,0},{6,4}} | collective-permute-start | bytes 11403272 | tf_op jit(solution)/shard_map/ppermute | solution.py:577
  1002.5 60.4 %collective-permute-start.2 = (bf16[5888,256]{1,0:T(8,128)(2,1)}, bf16[5888,256]{1,0:T(8,128)(2,1)S(1)}, u32[]{:S(2)}, u32[]{:S(2)}) collective-permute-start(bf16[5888,256]{1,0:T(8,128)(2,1)} %get-tuple-element.31), channel_id=1, source_target_pairs={{3,1},{7,5}} | collective-permute-start | bytes 9043976 | tf_op jit(solution)/shard_map/ppermute | solution.py:578
  1003.4 80.9 %collective-permute-start = (bf16[256,256]{1,0:T(8,128)(2,1)}, bf16[256,256]{1,0:T(8,128)(2,1)S(1)}, u32[]{:S(2)}, u32[]{:S(2)}) collective-permute-start(bf16[256,256]{1,0:T(8,128)(2,1)} %get-tuple-element.29), channel_id=1, source_target_pairs={{2,0},{3,1},{6,4},{7,5}} | collective-permute-start | bytes 393224 | tf_op jit(solution)/shard_map/ppermute | solution.py:579
  1004.7 0.8 copy-start
  1005.5 0.7 copy-start.1

commit v8 on v7

--- a/solution.py
+++ b/solution.py
@@ -512,13 +512,11 @@
 
 def last_kernel(late_c, old, out, sem):
     me = lax.axis_index("a")
-
-    @pl.when(me < 2)
-    def _():
-        place = pl.multiple_of((me + 3) * BLOCK - LAST, LAST)
-        copy = pltpu.make_async_copy(late_c, out.at[ROWS - 1, 0, pl.ds(place, LAST)], sem)
-        copy.start()
-        copy.wait()
+    far = me // 2
+    place = pl.multiple_of((1 - far) * ((me + 3) * BLOCK - LAST) + far * (SEQ + CACHE_ROOM - LAST), LAST)
+    copy = pltpu.make_async_copy(late_c, out.at[ROWS - 1, 0, pl.ds(place, LAST)], sem)
+    copy.start()
+    copy.wait()
 
 
 def trig_table():

time: 1090 us -> 1090 us (level)
  no operation moved by 1% of the time
where the time goes in v8:
time: 1090 us; the launch traced here: 1080 us
  Pallas kernels  1060 us (97%)
  waiting for transfers between devices  19.5 us (2%)
    pallas_call x1, Pallas kernels, device_step(): pl.pallas_call(move_kernel, out_shape=(loc_land, loc_land, glo_land, glo_...  1000 us
    pallas_call x1, Pallas kernels, device_step(): pl.pallas_call(write_kernel, out_shape=(jax.ShapeDtypeStruct((ROWS, model...  56.7 us
  transfers between devices with their start and end apart: 3, of which 2 were waited for; matrix products, arithmetic and copies ran while one was open for 0% of the time, Pallas kernels for 5%

profile of v8, /device:TPU:0, one launch (start us, length us, event | category | flops | bytes accessed | tf_op | source)
XLA Modules:
  0.0 1085.0 jit_solution(11876452825269257325)
XLA Ops:
  0.6 1000.6 %shard_map.209 = (bf16[8,1,4096,256]{3,2,1,0:T(8,128)(2,1)}, bf16[8,1,4096,256]{3,2,1,0:T(8,128)(2,1)}, bf16[8,1,6144,256]{3,2,1,0:T(8,128)(2,1)}, bf16[8,1,6144...) custom-call(bf16[8,2560]{1,0:T(8,128)(2,1)} %hid_in.1, ...), custom_call_target="tpu_custom_call" | custom-call | tf_op jit(solution)/shard_map/pallas_call | solution.py:546
  1001.2 1.3 collective-permute-start.1
  1002.5 0.9 collective-permute-start.2
  1003.4 1.3 collective-permute-start
  1004.7 0.0 copy-start
  1004.7 0.8 copy-done
  1005.5 0.0 copy-start.1
  1005.5 0.7 copy-done.1
  1006.2 56.7 %shard_map.210 = (bf16[8,2560]{1,0:T(8,128)(2,1)}, bf16[8,1,4096,256]{3,2,1,0:T(8,128)(2,1)}, bf16[8,1,4096,256]{3,2,1,0:T(8,128)(2,1)}, bf16[8,1,6656,256]{3,2,1,0:T(8,128)(2,1)}, bf16[8,1,6656,256]{3,2,1,0:T(8,128)(2,1)}) custom-call(bf16[8,2560]{1,0:T(8,128)(2,1)S(1)} %copy-done, bf16[4,8,256]{2,1,0:T(8,128)(2,1)S(1)} %copy-done.1, ...), custom_call_target="tpu_custom_call" | custom-call | flops 1000000000 | bytes 180000000 | tf_op jit(solution)/shard_map/pallas_call | solution.py:578
  1062.9 0.0 collective-permute-done.2.late_b
  1062.9 18.6 %collective-permute-done.1.late_a = bf16[7424,256]{1,0:T(8,128)(2,1)S(1)} collective-permute-done((bf16[7424,256]{1,0:T(8,128)(2,1)}, bf16[7424,256]{1,0:T(8,128)(2,1)S(1)}, u32[]{:S(2)}, u32[]{:S(2)}) %collective-permute-start.1) | collective-permute-done | bytes 3801120 | tf_op jit(solution)/shard_map/ppermute | solution.py:575
  1081.5 1.9 shard_map.211.old
  1083.4 0.9 collective-permute-done.late_c
  1084.3 0.7 shard_map.212
Async XLA Ops:
  1001.2 80.3 %collective-permute-start.1 = (bf16[7424,256]{1,0:T(8,128)(2,1)}, bf16[7424,256]{1,0:T(8,128)(2,1)S(1)}, u32[]{:S(2)}, u32[]{:S(2)}) collective-permute-start(bf16[7424,256]{1,0:T(8,128)(2,1)} %get-tuple-element.30), channel_id=1, source_target_pairs={{2,0},{6,4}} | collective-permute-start | bytes 11403272 | tf_op jit(solution)/shard_map/ppermute | solution.py:575
  1002.5 60.4 %collective-permute-start.2 = (bf16[5888,256]{1,0:T(8,128)(2,1)}, bf16[5888,256]{1,0:T(8,128)(2,1)S(1)}, u32[]{:S(2)}, u32[]{:S(2)}) collective-permute-start(bf16[5888,256]{1,0:T(8,128)(2,1)} %get-tuple-element.31), channel_id=1, source_target_pairs={{3,1},{7,5}} | collective-permute-start | bytes 9043976 | tf_op jit(solution)/shard_map/ppermute | solution.py:576
  1003.4 80.9 %collective-permute-start = (bf16[256,256]{1,0:T(8,128)(2,1)}, bf16[256,256]{1,0:T(8,128)(2,1)S(1)}, u32[]{:S(2)}, u32[]{:S(2)}) collective-permute-start(bf16[256,256]{1,0:T(8,128)(2,1)} %get-tuple-element.29), channel_id=1, source_target_pairs={{2,0},{3,1},{6,4},{7,5}} | collective-permute-start | bytes 393224 | tf_op jit(solution)/shard_map/ppermute | solution.py:577
  1004.7 0.8 copy-start
  1005.5 0.7 copy-start.1

commit v9 on v7

--- a/solution.py
+++ b/solution.py
@@ -29,7 +29,7 @@
 PIECES = 8
 WO_ROWS = 64
 LAST = 256
-FIRST = 16
+FIRST = 8
 STAT = 64
 LOW = -1e30
 

time: 1090 us -> 1090 us (level)
  no operation moved by 1% of the time
where the time goes in v9:
time: 1090 us; the launch traced here: 1080 us
  Pallas kernels  1060 us (97%)
  waiting for transfers between devices  19.5 us (2%)
    pallas_call x1, Pallas kernels, device_step(): pl.pallas_call(move_kernel, out_shape=(loc_land, loc_land, glo_land, glo_...  1000 us
    pallas_call x1, Pallas kernels, device_step(): pl.pallas_call(write_kernel, out_shape=(jax.ShapeDtypeStruct((ROWS, model...  56.7 us
  transfers between devices with their start and end apart: 3, of which 2 were waited for; matrix products, arithmetic and copies ran while one was open for 0% of the time, Pallas kernels for 5%

profile of v9, /device:TPU:0, one launch (start us, length us, event | category | flops | bytes accessed | tf_op | source)
XLA Modules:
  0.0 1085.0 jit_solution(10543378361379322540)
XLA Ops:
  0.6 1000.6 %shard_map.209 = (bf16[8,1,4096,256]{3,2,1,0:T(8,128)(2,1)}, bf16[8,1,4096,256]{3,2,1,0:T(8,128)(2,1)}, bf16[8,1,6144,256]{3,2,1,0:T(8,128)(2,1)}, bf16[8,1,6144...) custom-call(bf16[8,2560]{1,0:T(8,128)(2,1)} %hid_in.1, ...), custom_call_target="tpu_custom_call" | custom-call | tf_op jit(solution)/shard_map/pallas_call | solution.py:548
  1001.2 1.3 collective-permute-start.1
  1002.5 0.9 collective-permute-start.2
  1003.4 1.3 collective-permute-start
  1004.7 0.0 copy-start
  1004.7 0.8 copy-done
  1005.5 0.0 copy-start.1
  1005.5 0.7 copy-done.1
  1006.2 56.7 %shard_map.210 = (bf16[8,2560]{1,0:T(8,128)(2,1)}, bf16[8,1,4096,256]{3,2,1,0:T(8,128)(2,1)}, bf16[8,1,4096,256]{3,2,1,0:T(8,128)(2,1)}, bf16[8,1,6656,256]{3,2,1,0:T(8,128)(2,1)}, bf16[8,1,6656,256]{3,2,1,0:T(8,128)(2,1)}) custom-call(bf16[8,2560]{1,0:T(8,128)(2,1)S(1)} %copy-done, bf16[4,8,256]{2,1,0:T(8,128)(2,1)S(1)} %copy-done.1, ...), custom_call_target="tpu_custom_call" | custom-call | flops 1000000000 | bytes 180000000 | tf_op jit(solution)/shard_map/pallas_call | solution.py:580
  1062.9 0.0 collective-permute-done.2.late_b
  1062.9 18.6 %collective-permute-done.1.late_a = bf16[7424,256]{1,0:T(8,128)(2,1)S(1)} collective-permute-done((bf16[7424,256]{1,0:T(8,128)(2,1)}, bf16[7424,256]{1,0:T(8,128)(2,1)S(1)}, u32[]{:S(2)}, u32[]{:S(2)}) %collective-permute-start.1) | collective-permute-done | bytes 3801120 | tf_op jit(solution)/shard_map/ppermute | solution.py:577
  1081.5 1.9 shard_map.211.old
  1083.4 0.9 collective-permute-done.late_c
  1084.3 0.7 shard_map.212
Async XLA Ops:
  1001.2 80.3 %collective-permute-start.1 = (bf16[7424,256]{1,0:T(8,128)(2,1)}, bf16[7424,256]{1,0:T(8,128)(2,1)S(1)}, u32[]{:S(2)}, u32[]{:S(2)}) collective-permute-start(bf16[7424,256]{1,0:T(8,128)(2,1)} %get-tuple-element.30), channel_id=1, source_target_pairs={{2,0},{6,4}} | collective-permute-start | bytes 11403272 | tf_op jit(solution)/shard_map/ppermute | solution.py:577
  1002.5 60.4 %collective-permute-start.2 = (bf16[5888,256]{1,0:T(8,128)(2,1)}, bf16[5888,256]{1,0:T(8,128)(2,1)S(1)}, u32[]{:S(2)}, u32[]{:S(2)}) collective-permute-start(bf16[5888,256]{1,0:T(8,128)(2,1)} %get-tuple-element.31), channel_id=1, source_target_pairs={{3,1},{7,5}} | collective-permute-start | bytes 9043976 | tf_op jit(solution)/shard_map/ppermute | solution.py:578
  1003.4 80.9 %collective-permute-start = (bf16[256,256]{1,0:T(8,128)(2,1)}, bf16[256,256]{1,0:T(8,128)(2,1)S(1)}, u32[]{:S(2)}, u32[]{:S(2)}) collective-permute-start(bf16[256,256]{1,0:T(8,128)(2,1)} %get-tuple-element.29), channel_id=1, source_target_pairs={{2,0},{3,1},{6,4},{7,5}} | collective-permute-start | bytes 393224 | tf_op jit(solution)/shard_map/ppermute | solution.py:579
  1004.7 0.8 copy-start
  1005.5 0.7 copy-start.1
